TPU v7x, 512 devices: a whole 4x4x16 slice. The times are simulated.
512 devices in a mesh: dp: 32 (over z_hi, y, core), seq: 16 (over x, z_lo).
Axes of the slice: x: 4, y: 4, z: 16 (z_hi: 4, z_lo: 4; z = z_hi * 4 + z_lo), core: 2. Of those that a mesh axis runs over, the one named last changes fastest.
Arguments:
- features: bfloat16 [32, 4096, 1024], P('dp', 'seq'), may hold values from -6 to 6
- shift_offsets: int32 [16], replicated, may hold values from -4 to 4, as said below
- conv_weight: bfloat16 [3, 1024, 1024], P(None, None, 'dp'), may hold values from -0.109375 to 0.109375
- norm_gain: float32 [1024], replicated, may hold values from 0.5 to 1.5
- query_proj: bfloat16 [32, 512, 512], P('dp', 'seq'), may hold values from -6 to 6
- key_proj: bfloat16 [32, 512, 512], P('dp', 'seq'), may hold values from -6 to 6
- value_proj: bfloat16 [32, 512, 768], P('dp', 'seq'), may hold values from -6 to 6
- head_weight: bfloat16 [1792, 512], replicated, may hold values from -0.125 to 0.125
- targets: float32 [32, 512, 512], P('dp', 'seq'), may hold values from 0 to 3
- track_mask: int32 [16, 512], replicated, may hold values from 0 to 1, as said below
- track_pairing: int32 [512], replicated, may hold values from 0 to 511, as said below
Outputs:
- features_grad: bfloat16 [32, 4096, 1024], P('dp', 'seq')
- query_grad: bfloat16 [32, 512, 512], P('dp', 'seq')
- key_grad: bfloat16 [32, 512, 512], P('dp', 'seq')
- value_grad: bfloat16 [32, 512, 768], P('dp', 'seq')
- gain_grad: float32 [1024], replicated
- mean_loss: float32 [], replicated
Inputs may be any that keep to these rules, and one draw needn't show every extreme that they name: `shift_offsets`: offset in positions of each interval's 16-bp input. `track_mask`: 1 where the interval has data for the track. `track_pairing`: A pairing: applied twice it gives every track back.
All inputs are finite; a program needn't handle non-finite values.
Results may differ from a plain program's by a relative error of at most 0.028.
Values may be sent and summed in bfloat16 or wider, within the bound.
A program may use at most 64 MiB of HBM per device.

v0:
```python
import math

import jax
import jax.numpy as jnp
from jax import lax
from jax.sharding import PartitionSpec as P

KW = 3
SHIFT = 4
POOL = 8
HEADS = 4
QK = 128
VD = 192


NORM_EPS = 1e-06
LOSS_SCALE = 1024.0


def with_halo(block, sides, width):
    for axis, dim in sides:
        count = lax.axis_size(axis)
        forward = [(i, i + 1) for i in range(count - 1)]
        backward = [(target, source) for source, target in forward]
        low = lax.ppermute(
            lax.slice_in_dim(block, block.shape[dim] - width, None, axis=dim), axis, forward
        )
        high = lax.ppermute(lax.slice_in_dim(block, 0, width, axis=dim), axis, backward)
        block = jnp.concatenate([low, block, high], axis=dim)
    return block


def swapped(value, axis, apart):
    mask = 2**apart
    pairs = [(source, source ^ mask) for source in range(lax.axis_size(axis))]
    return lax.ppermute(value, axis, pairs)


def residual_terms(own_pred, theirs, wanted, mask_row, track_pairing):
    misfit = 0.5 * (own_pred + jnp.take(theirs, track_pairing, axis=1)) - wanted
    return (mask_row * misfit, misfit)


def body(
    features,
    shift_offsets,
    conv_weight,
    norm_gain,
    query_proj,
    key_proj,
    value_proj,
    head_weight,
    targets,
    track_mask,
    track_pairing,
):
    feats_local = features[0]
    pos_rows = feats_local.shape[0]
    channels = feats_local.shape[1]
    half_taps = KW // 2
    strand_idx = lax.axis_index("dp")
    strands = lax.axis_size("dp")
    pairs_count = strands // 2
    interval = strand_idx % pairs_count
    flipped = strand_idx >= pairs_count
    chosen = lax.dynamic_index_in_dim(shift_offsets, interval, 0, keepdims=False)
    offset = jnp.where(flipped, -chosen, chosen)
    seq_idx = lax.axis_index("seq")
    seq_count = lax.axis_size("seq")
    full_weight = lax.all_gather(conv_weight, "dp", axis=2, tiled=True)
    rim_width = SHIFT + half_taps
    extended = with_halo(feats_local, (("seq", 0),), rim_width)
    shifted = lax.dynamic_slice_in_dim(extended, SHIFT - offset, pos_rows + 2 * half_taps, 0)
    source = shifted.astype(jnp.float32)
    inv_rms = lax.rsqrt(jnp.mean(source * source, axis=1, keepdims=True) + NORM_EPS)
    normed = source * inv_rms
    gained = normed * norm_gain
    global_pos = seq_idx * pos_rows - half_taps + lax.iota(jnp.int32, pos_rows + 2 * half_taps)
    inside = (global_pos >= 0) & (global_pos < seq_count * pos_rows)
    hidden = jnp.where(inside[:, None], jax.nn.gelu(gained), 0.0).astype(jnp.bfloat16)
    conv_out = jnp.zeros((pos_rows, channels), jnp.float32)
    for tap_idx in range(KW):
        tap_pick = jnp.where(flipped, KW - 1 - tap_idx, tap_idx).astype(jnp.int32)
        weight_tap = lax.dynamic_index_in_dim(full_weight, tap_pick, 0, keepdims=False)
        conv_out = conv_out + jnp.dot(
            hidden[tap_idx : tap_idx + pos_rows], weight_tap, preferred_element_type=jnp.float32
        )
    own_source = source[half_taps : half_taps + pos_rows]
    output = lax.optimization_barrier((own_source + conv_out).astype(jnp.bfloat16))
    tokens = pos_rows // POOL
    pooled = jnp.mean(output.astype(jnp.float32).reshape(tokens, POOL, channels), axis=1).astype(
        jnp.bfloat16
    )
    all_keys, all_values = (
        lax.all_gather(key_proj[0], "seq", axis=0, tiled=True),
        lax.all_gather(value_proj[0], "seq", axis=0, tiled=True),
    )
    key_count = all_keys.shape[0]
    query_h = query_proj[0].reshape(tokens, HEADS, QK)
    key_h = all_keys.reshape(key_count, HEADS, QK)
    value_h = all_values.reshape(key_count, HEADS, VD)
    inv_sqrt = 1.0 / math.sqrt(QK)
    scores = (
        jnp.einsum("thd,lhd->htl", query_h, key_h, preferred_element_type=jnp.float32) * inv_sqrt
    )
    row_max = jnp.max(scores, axis=2, keepdims=True)
    exp_scores = jnp.exp(scores - row_max)
    totals = jnp.sum(exp_scores, axis=2, keepdims=True)
    soft_f32 = exp_scores / totals
    soft_b16 = soft_f32.astype(jnp.bfloat16)
    attended = (
        jnp.einsum("htl,lhd->thd", soft_b16, value_h, preferred_element_type=jnp.float32)
        .reshape(tokens, HEADS * VD)
        .astype(jnp.bfloat16)
    )
    joined = jnp.concatenate([pooled, attended], axis=1)
    logits = jnp.dot(joined, head_weight, preferred_element_type=jnp.float32)
    predicted = jax.nn.softplus(logits)
    mask_row = lax.dynamic_index_in_dim(track_mask, interval, 0, keepdims=False).astype(jnp.float32)
    counted = jnp.maximum(jnp.sum(mask_row), 1.0)
    mirror_bit = strands.bit_length() - 2
    wanted_own = targets[0]
    partner_pred = swapped(predicted, "dp", mirror_bit)
    weighted, misfit = residual_terms(predicted, partner_pred, wanted_own, mask_row, track_pairing)
    slopes = 2.0 * LOSS_SCALE * weighted / counted
    partner_slope = swapped(slopes, "dp", mirror_bit)
    dpredicted = 0.5 * (slopes + jnp.take(partner_slope, track_pairing, axis=1))
    loss_part = jnp.sum(weighted * misfit / counted) / (strands * tokens * seq_count)
    dlogit = (dpredicted * jax.nn.sigmoid(logits)).astype(jnp.bfloat16)
    djoined = lax.dot_general(
        dlogit, head_weight, (((1,), (1,)), ((), ())), preferred_element_type=jnp.float32
    )
    dpooled = djoined[:, :channels]
    dattended = djoined[:, channels:].astype(jnp.bfloat16)
    dout_h = dattended.reshape(tokens, HEADS, VD)
    row_dots = jnp.sum(
        dout_h.astype(jnp.float32) * attended.reshape(tokens, HEADS, VD).astype(jnp.float32), axis=2
    )
    dprobs = jnp.einsum("thd,lhd->htl", dout_h, value_h, preferred_element_type=jnp.float32)
    dscore = (soft_f32 * (dprobs - row_dots.T[:, :, None])).astype(jnp.bfloat16)
    query_grad = (
        (jnp.einsum("htl,lhd->thd", dscore, key_h, preferred_element_type=jnp.float32) * inv_sqrt)
        .reshape(tokens, HEADS * QK)
        .astype(jnp.bfloat16)
    )
    key_part = jnp.einsum(
        "htl,thd->lhd", dscore, query_h, preferred_element_type=jnp.float32
    ).reshape(tokens * lax.axis_size("seq"), HEADS * QK)
    value_part = jnp.einsum(
        "htl,thd->lhd", soft_b16, dout_h, preferred_element_type=jnp.float32
    ).reshape(tokens * lax.axis_size("seq"), HEADS * VD)
    summed = lax.psum_scatter(
        jnp.concatenate([key_part, value_part], axis=1).astype(jnp.bfloat16),
        "seq",
        scatter_dimension=0,
        tiled=True,
    ).astype(jnp.float32)
    key_grad = (summed[:, : HEADS * QK] * inv_sqrt).astype(jnp.bfloat16)
    value_grad = summed[:, HEADS * QK :].astype(jnp.bfloat16)
    dgrad_f32 = jnp.broadcast_to((dpooled / POOL)[:, None, :], (tokens, POOL, channels)).reshape(
        pos_rows, channels
    )
    dgrad_b = dgrad_f32.astype(jnp.bfloat16)
    dgrad_ext = with_halo(dgrad_b, (("seq", 0),), half_taps)
    dhidden = jnp.zeros((pos_rows, channels), jnp.float32)
    for tap_idx in range(KW):
        tap_pick = jnp.where(flipped, KW - 1 - tap_idx, tap_idx).astype(jnp.int32)
        weight_tap = lax.dynamic_index_in_dim(full_weight, tap_pick, 0, keepdims=False)
        tap_start = KW - 1 - tap_idx
        dhidden = dhidden + lax.dot_general(
            dgrad_ext[tap_start : tap_start + pos_rows],
            weight_tap,
            (((1,), (1,)), ((), ())),
            preferred_element_type=jnp.float32,
        )
    own_gained = gained[half_taps : half_taps + pos_rows]
    own_normed = normed[half_taps : half_taps + pos_rows]
    own_inv = inv_rms[half_taps : half_taps + pos_rows]
    unused_out, gelu_back = jax.vjp(jax.nn.gelu, own_gained)
    dgained = gelu_back(dhidden)[0]
    gain_part = jnp.sum(dgained * own_normed, axis=0)
    dnormed = dgained * norm_gain
    dsource = (
        own_inv * (dnormed - own_normed * jnp.mean(dnormed * own_normed, axis=1, keepdims=True))
        + dgrad_f32
    )
    dsource_b = dsource.astype(jnp.bfloat16)
    dsource_ext = with_halo(dsource_b, (("seq", 0),), SHIFT)
    features_grad = lax.dynamic_slice_in_dim(dsource_ext, SHIFT + offset, pos_rows, 0)
    gain_grad, mean_loss = lax.psum((gain_part, loss_part), ("dp", "seq"))
    return (
        features_grad[None],
        query_grad[None],
        key_grad[None],
        value_grad[None],
        gain_grad,
        mean_loss,
    )


def solution(mesh):
    placed = (
        P("dp", "seq", None),
        P(),
        P(None, None, "dp"),
        P(),
        P("dp", "seq", None),
        P("dp", "seq", None),
        P("dp", "seq", None),
        P(),
        P("dp", "seq", None),
        P(),
        P(),
    )
    return jax.shard_map(
        body,
        mesh=mesh,
        in_specs=placed,
        out_specs=(
            P("dp", "seq", None),
            P("dp", "seq", None),
            P("dp", "seq", None),
            P("dp", "seq", None),
            P(),
            P(),
        ),
        check_vma=False,
    )
```

profile of v0, /device:TPU:1, one launch (start us, length us, event | category | flops | bytes accessed | tf_op | source)
XLA Modules:
  0.0 356.6 jit_solution(8261257887968308667)
XLA Ops:
  7.2 0.0 all-gather.4.cloned.1.call-start
  7.2 0.7 all-gather.4.cloned.1.call-update
  7.9 0.0 reduce-scatter.2.cloned.1.call-start
  8.0 1.4 slice_bitcast_fusion.5
  9.3 4.3 %collective-permute-start = (bf16[5,1024]{1,0:T(8,128)(2,1)}, bf16[5,1024]{1,0:T(8,128)(2,1)S(1)}, u32[]{:S(2)}, u32[]{:S(2)}) collective-permute-start(bf16[5,1024]{1,0:T(8,128)(2,1)} %get-tuple-element.24), channel_id=1, source_target_pairs={{0,1},{1,2},{2,3},{3,4},{4,5},{5,6},{6,7},{7,8},{8,9},{9,10},{10,1... | collective-permute-start | bytes 30728 | tf_op jit(solution)/shard_map/ppermute | solution.py:25
  13.7 1.3 collective-permute-start.1
  15.0 47.9 %all-gather = bf16[1,512,512]{2,1,0:T(8,128)(2,1)S(1)} all-gather(bf16[1,32,512]{2,1,0:T(8,128)(2,1)} %param.18), channel_id=2, replica_groups=mesh['dp'=32,'seq'=16] {'seq'}, dimensions={1}, use_global_device_ids=true | all-gather | bytes 557056 | tf_op jit(solution)/shard_map/all_gather | solution.py:95
  62.9 0.2 copy.43
  63.1 77.4 %all-gather.1 = bf16[1,512,768]{2,1,0:T(8,128)(2,1)S(1)} all-gather(bf16[1,32,768]{2,1,0:T(8,128)(2,1)S(1)} %copy-done.11), channel_id=3, replica_groups=mesh['dp'=32,'seq'=16] {'seq'}, dimensions={1}, use_global_device_ids=true | all-gather | bytes 835584 | tf_op jit(solution)/shard_map/all_gather | solution.py:96
  140.5 1.2 copy.46
  141.7 1.5 fusion.110
  143.2 0.5 compare_and_fusion
  143.6 0.2 convolution_multiply_fusion
  143.8 0.8 fusion.115
  144.7 0.6 copy-done.16
  145.3 0.4 fusion.31
  145.7 0.6 fusion.100
  146.3 0.6 dynamic_slice.27
  148.1 0.1 copy.47
  148.2 0.7 convert_element_type.88
  149.7 1.5 multiply_reduce_fusion
  151.2 1.9 fusion.42
  153.1 2.6 fusion.10
  155.7 2.3 fusion.3
  158.1 2.5 fusion.50
  160.6 0.3 convert_reduce_fusion
  161.0 0.5 compare_select_fusion
  161.4 16.5 %collective-permute-start.2 = (f32[32,512]{1,0:T(8,128)S(1)}, f32[32,512]{1,0:T(8,128)S(1)}, u32[]{:S(2)}, u32[]{:S(2)}) collective-permute-start(f32[32,512]{1,0:T(8,128)S(1)} %get-tuple-element.30), channel_id=1, source_target_pairs={{0,256},{16,272},{32,288},{48,304},{64,320},{80,336},{96,352},{112... | collective-permute-start | bytes 196616 | tf_op jit(solution)/shard_map/ppermute | solution.py:36
  177.9 1.6 collective-permute-done.2
  179.5 0.1 copy.48
  179.7 1.0 gather_fusion
  180.7 0.1 copy.49
  180.8 0.7 fusion.81
  181.5 12.1 %collective-permute-start.3 = (f32[32,512]{1,0:T(8,128)S(1)}, f32[32,512]{1,0:T(8,128)S(1)}, u32[]{:S(2)}, u32[]{:S(2)}) collective-permute-start(f32[32,512]{1,0:T(8,128)S(1)} %fusion.75), channel_id=1, source_target_pairs={{0,256},{16,272},{32,288},{48,304},{64,320},{80,336},{96,352},{112... | collective-permute-start | bytes 196616 | tf_op jit(solution)/shard_map/ppermute | solution.py:36
  193.6 0.1 slice.76
  194.3 1.2 collective-permute-done.3
  195.5 0.1 copy.50
  195.7 1.0 gather_fusion.1
  196.7 0.1 copy.51
  196.8 0.6 fusion.85
  197.5 0.1 reshape.106
  197.6 1.0 multiply_reduce_fusion.3
  198.6 2.4 convolution_convert_fusion
  201.0 1.2 fusion.30
  202.3 0.3 convolution_convert_fusion.1
  202.6 1.0 copy.58
  203.6 1.4 copy.59
  205.0 2.2 pad_maximum_fusion
  207.2 0.0 reduce-scatter.2.cloned.1.call-update
  207.3 0.1 bitcast_convert_fusion
  207.4 3.5 collective-permute-start.5
  210.8 1.3 collective-permute-start.4
  212.1 2.3 fusion.9
  214.5 2.5 fusion.1
  217.0 3.3 multiply_reduce_fusion.1
  220.3 0.4 fusion.49
  220.7 4.0 %collective-permute-start.6 = (bf16[4,1024]{1,0:T(4,128)(2,1)S(1)}, bf16[4,1024]{1,0:T(4,128)(2,1)S(1)}, u32[]{:S(2)}, u32[]{:S(2)}) collective-permute-start(bf16[4,1024]{1,0:T(4,128)(2,1)S(1)} %get-tuple-element.21), channel_id=1, source_target_pairs={{0,1},{1,2},{2,3},{3,4},{4,5},{5,6},{6,7},{7,8},{8,9},{9,10},{10,1... | collective-permute-start | bytes 24584 | tf_op jit(solution)/shard_map/ppermute | solution.py:25
  224.7 1.3 collective-permute-start.7
  226.0 0.3 fusion.33
  226.3 0.6 convert_element_type.99
  226.9 118.9 %all-reduce = (f32[1024]{0:T(1024)}, f32[]{:T(128)}) all-reduce(f32[1024]{0:T(1024)S(1)} %get-tuple-element.7, f32[]{:T(128)S(6)} %div.54), channel_id=1, replica_groups=mesh['dp'=32,'seq'=16] {'dp','seq'}, use_global_device_ids=true, to_apply=%region_9.11 | all-reduce | flops 1025 | bytes 8200 | tf_op jit(solution)/shard_map/psum | solution.py:190
  345.8 1.2 fusion.58
  347.0 1.4 slice_bitcast_fusion.3
  348.4 1.4 fusion.84
  (59 shorter events, 0.3 us)
Async XLA Ops:
  7.2 153.7 %copy-start = (bf16[1792,512]{1,0:T(8,128)(2,1)S(1)}, bf16[1792,512]{1,0:T(8,128)(2,1)}, u32[]{:S(2)}) copy-start(bf16[1792,512]{1,0:T(8,128)(2,1)} %param.20) | copy-start | bytes 5505028
  7.2 55.9 %copy-start.12 = (bf16[1,32,512]{2,1,0:T(8,128)(2,1)S(1)}, bf16[1,32,512]{2,1,0:T(8,128)(2,1)}, u32[]{:S(2)}) copy-start(bf16[1,32,512]{2,1,0:T(8,128)(2,1)} %param.17) | copy-start | bytes 98308
  7.2 56.0 %copy-start.11 = (bf16[1,32,768]{2,1,0:T(8,128)(2,1)S(1)}, bf16[1,32,768]{2,1,0:T(8,128)(2,1)}, u32[]{:S(2)}) copy-start(bf16[1,32,768]{2,1,0:T(8,128)(2,1)} %param.19) | copy-start | bytes 147460
  7.2 145.9 %all-gather.4.cloned.1.call-start = ((), (), s32[]{:S(2)}) async-start(), calls=%async_computation.1 | async-start | bytes 6488064 | tf_op jit(solution)/shard_map/all_gather | solution.py:70
  7.9 339.1 %reduce-scatter.2.cloned.1.call-start = ((), (), s32[]{:S(2)}) async-start(), calls=%async_computation.2 | async-start | bytes 1392640 | tf_op jit(solution)/shard_map/reduce_scatter | solution.py:152
  9.3 140.3 %collective-permute-start = (bf16[5,1024]{1,0:T(8,128)(2,1)}, bf16[5,1024]{1,0:T(8,128)(2,1)S(1)}, u32[]{:S(2)}, u32[]{:S(2)}) collective-permute-start(bf16[5,1024]{1,0:T(8,128)(2,1)} %get-tuple-element.24), channel_id=1, source_target_pairs={{0,1},{1,2},{2,3},{3,4},{4,5},{5,6},{6,7},{7,8},{8,9},{9,10},{10,1... | collective-permute-start | bytes 30728 | tf_op jit(solution)/shard_map/ppermute | solution.py:25
  13.7 135.9 %collective-permute-start.1 = (bf16[5,1024]{1,0:T(8,128)(2,1)}, bf16[5,1024]{1,0:T(8,128)(2,1)S(1)}, u32[]{:S(2)}, u32[]{:S(2)}) collective-permute-start(bf16[5,1024]{1,0:T(8,128)(2,1)} %get-tuple-element.25), channel_id=1, source_target_pairs={{1,0},{2,1},{3,2},{4,3},{5,4},{6,5},{7,6},{8,7},{9,8},{10,9},{11,1... | collective-permute-start | bytes 30728 | tf_op jit(solution)/shard_map/ppermute | solution.py:28
  63.1 80.0 %copy-start.14 = (s32[512]{0:T(512)S(1)}, s32[512]{0:T(512)}, u32[]{:S(2)}) copy-start(s32[512]{0:T(512)} %param.23) | copy-start | bytes 6148
  141.7 3.6 %copy-start.5 = (bf16[1,512,768]{1,2,0:T(8,128)(2,1)S(1)}, bf16[1,512,768]{1,2,0:T(8,128)(2,1)}, u32[]{:S(2)}) copy-start(bf16[1,512,768]{1,2,0:T(8,128)(2,1)} %copy.46) | copy-start | bytes 2359300
  143.6 2.6 copy-start.19
  143.8 5.8 %copy-start.4 = (f32[4,32,512]{2,1,0:T(8,128)}, f32[4,32,512]{2,1,0:T(8,128)S(1)}, u32[]{:S(2)}) copy-start(f32[4,32,512]{2,1,0:T(8,128)S(1)} %convolution_multiply_fusion) | copy-start | bytes 786436
  144.7 0.6 copy-start.16
  145.6 4.0 %copy-start.8 = (bf16[32,4,192]{2,0,1:T(8,128)(2,1)}, bf16[32,4,192]{2,0,1:T(8,128)(2,1)S(1)}, u32[]{:S(2)}) copy-start(bf16[32,4,192]{2,0,1:T(8,128)(2,1)S(1)} %fusion.31) | copy-start | bytes 147460
  145.6 5.6 %copy-start.13 = (f32[1024]{0:T(1024)S(1)}, f32[1024]{0:T(1024)}, u32[]{:S(2)}) copy-start(f32[1024]{0:T(1024)} %param.16) | copy-start | bytes 12292
  149.6 1.6 copy-start.18
  153.1 2.6 copy-start.2
  158.0 2.9 copy-start.9
  160.9 19.9 %copy-start.10 = (f32[1,32,512]{2,1,0:T(8,128)S(1)}, f32[1,32,512]{2,1,0:T(8,128)}, u32[]{:S(2)}) copy-start(f32[1,32,512]{2,1,0:T(8,128)} %param.21) | copy-start | bytes 196612
  160.9 19.9 %copy-start.15 = (pred[512]{0:T(512)(128)(4,1)S(1)}, pred[512]{0:T(512)(128)(4,1)}, u32[]{:S(2)}) copy-start(pred[512]{0:T(512)(128)(4,1)} %compare_and_fusion) | copy-start | bytes 1540
  161.4 18.1 %collective-permute-start.2 = (f32[32,512]{1,0:T(8,128)S(1)}, f32[32,512]{1,0:T(8,128)S(1)}, u32[]{:S(2)}, u32[]{:S(2)}) collective-permute-start(f32[32,512]{1,0:T(8,128)S(1)} %get-tuple-element.30), channel_id=1, source_target_pairs={{0,256},{16,272},{32,288},{48,304},{64,320},{80,336},{96,352},{112... | collective-permute-start | bytes 196616 | tf_op jit(solution)/shard_map/ppermute | solution.py:36
  181.5 14.0 %collective-permute-start.3 = (f32[32,512]{1,0:T(8,128)S(1)}, f32[32,512]{1,0:T(8,128)S(1)}, u32[]{:S(2)}, u32[]{:S(2)}) collective-permute-start(f32[32,512]{1,0:T(8,128)S(1)} %fusion.75), channel_id=1, source_target_pairs={{0,256},{16,272},{32,288},{48,304},{64,320},{80,336},{96,352},{112... | collective-permute-start | bytes 196616 | tf_op jit(solution)/shard_map/ppermute | solution.py:36
  196.8 1.8 copy-start.17
  197.4 3.6 %copy-start.6 = (bf16[1,512,768]{1,2,0:T(8,128)(2,1)S(1)}, bf16[1,512,768]{1,2,0:T(8,128)(2,1)}, u32[]{:S(2)}) copy-start(bf16[1,512,768]{1,2,0:T(8,128)(2,1)} %copy.46) | copy-start | bytes 2359300
  197.6 3.4 copy-start.7
  207.4 7.1 %collective-permute-start.5 = (bf16[1,1024]{1,0:T(2,128)(2,1)S(1)}, bf16[1,1024]{1,0:T(2,128)(2,1)S(1)}, u32[]{:S(2)}, u32[]{:S(2)}) collective-permute-start(bf16[1,1024]{1,0:T(2,128)(2,1)S(1)} %get-tuple-element.23), channel_id=1, source_target_pairs={{0,1},{1,2},{2,3},{3,4},{4,5},{5,6},{6,7},{7,8},{8,9},{9,10},{10,1... | collective-permute-start | bytes 6152 | tf_op jit(solution)/shard_map/ppermute | solution.py:25
  210.8 6.1 %collective-permute-start.4 = (bf16[1,1024]{1,0:T(2,128)(2,1)S(1)}, bf16[1,1024]{1,0:T(2,128)(2,1)S(1)}, u32[]{:S(2)}, u32[]{:S(2)}) collective-permute-start(bf16[1,1024]{1,0:T(2,128)(2,1)S(1)} %get-tuple-element.22), channel_id=1, source_target_pairs={{1,0},{2,1},{3,2},{4,3},{5,4},{6,5},{7,6},{8,7},{9,8},{10,9},{11,1... | collective-permute-start | bytes 6152 | tf_op jit(solution)/shard_map/ppermute | solution.py:28
  214.4 2.5 copy-start.1
  214.5 2.5 copy-start.3
  220.7 125.1 %collective-permute-start.6 = (bf16[4,1024]{1,0:T(4,128)(2,1)S(1)}, bf16[4,1024]{1,0:T(4,128)(2,1)S(1)}, u32[]{:S(2)}, u32[]{:S(2)}) collective-permute-start(bf16[4,1024]{1,0:T(4,128)(2,1)S(1)} %get-tuple-element.21), channel_id=1, source_target_pairs={{0,1},{1,2},{2,3},{3,4},{4,5},{5,6},{6,7},{7,8},{8,9},{9,10},{10,1... | collective-permute-start | bytes 24584 | tf_op jit(solution)/shard_map/ppermute | solution.py:25
  224.7 121.1 %collective-permute-start.7 = (bf16[4,1024]{1,0:T(4,128)(2,1)S(1)}, bf16[4,1024]{1,0:T(4,128)(2,1)S(1)}, u32[]{:S(2)}, u32[]{:S(2)}) collective-permute-start(bf16[4,1024]{1,0:T(4,128)(2,1)S(1)} %get-tuple-element.20), channel_id=1, source_target_pairs={{1,0},{2,1},{3,2},{4,3},{5,4},{6,5},{7,6},{8,7},{9,8},{10,9},{11,1... | collective-permute-start | bytes 24584 | tf_op jit(solution)/shard_map/ppermute | solution.py:28
Sparse Core Ops, SparseCore 0:
  11.2 122.0 all-gather.3
  207.4 94.8 reduce-scatter.1
where the time goes:
time: 357 us
  blocking collectives  244 us (68%)
  starting transfers between devices  44.3 us (12%)
  matrix products  21.3 us (6%)
  between operations  17.2 us (5%)
  other arithmetic  14.1 us (4%)
  local copies, waits for them, and re-layouts  12.1 us (3%)
    psum x1, blocking collectives, body(): gain_grad, mean_loss = lax.psum((gain_part, loss_part), ('dp', 'seq'))  119 us
    all_gather x1, blocking collectives, body(): lax.all_gather(value_proj[0], 'seq', axis=0, tiled=True)  77.4 us
    all_gather x1, blocking collectives, body(): lax.all_gather(key_proj[0], 'seq', axis=0, tiled=True)  47.9 us
    ppermute x2, starting transfers between devices, swapped(): return lax.ppermute(value, axis, pairs)  28.5 us
    ppermute x3, starting transfers between devices, with_halo(): lax.ppermute(lax.slice_in_dim(block, block.shape[dim] - width, None, axis...  11.8 us
    dot_general x3, matrix products, body(): lax.dot_general(dgrad_ext[tap_start:tap_start + pos_rows], weight_tap, ((...  8.04 us
    dot_general x3, matrix products, body(): jnp.dot(hidden[tap_idx:tap_idx + pos_rows], weight_tap, preferred_element...  7.38 us
  transfers between devices with their start and end apart: 10, of which 2 were waited for; matrix products, arithmetic and copies ran while one was open for 6% of the time, Pallas kernels for 0%

commit v1 on v0

v1 whole, which is shorter than its diff:
```python
import math

import jax
import jax.numpy as jnp
from jax import lax
from jax.experimental import pallas as pl
from jax.experimental.pallas import tpu as pltpu
from jax.sharding import PartitionSpec as P

KW = 3
SHIFT = 4
POOL = 8
HEADS = 4
QK = 128
VD = 192
C = 1024
TRACKS = 512
ROWS = 256
TOK = 32
L16 = 4096
PAIRS = 16
RIM = 16
VP = 256
ROW = 1152
NORM_EPS = 1e-06
LOSS_SCALE = 1024.0
ROOT = math.sqrt(2.0 / math.pi)
CUBIC = 0.044715
COPIES = 136
f32 = jnp.float32
bf16 = jnp.bfloat16

NT = (((1,), (1,)), ((), ()))
NN = (((1,), (0,)), ((), ()))
TN = (((0,), (0,)), ((), ()))


def dot(a, b, dims):
    return lax.dot_general(a, b, dims, preferred_element_type=f32)


def iota(shape, axis):
    return lax.broadcasted_iota(jnp.int32, shape, axis)


class Copies:
    def __init__(self, send, recv):
        self.send, self.recv, self.used, self.sent = send, recv, 0, []

    def start(self, src, dst, device):
        n = self.used
        self.used += 1
        copy = pltpu.make_async_remote_copy(
            src_ref=src,
            dst_ref=dst,
            send_sem=self.send.at[n],
            recv_sem=self.recv.at[n],
            device_id=device,
            device_id_type=pl.DeviceIdType.MESH,
        )
        copy.start()
        self.sent.append(copy)
        return n

    def arrived(self, n, dst):
        pltpu.make_async_remote_copy(
            src_ref=dst,
            dst_ref=dst,
            send_sem=self.send.at[n],
            recv_sem=self.recv.at[n],
            device_id=self.someone,
            device_id_type=pl.DeviceIdType.MESH,
        ).wait_recv()

    def finish(self):
        for copy in self.sent:
            copy.wait_send()


class Gather:
    def __init__(self, copies, device, unit):
        self.copies, self.device, self.unit = copies, device, unit

    def begin(self):
        mine = self.unit(0, None)
        self.right = self.copies.start(mine, mine, self.device(1))
        self.left = self.copies.start(mine, mine, self.device(3))

    def relay(self):
        self.copies.arrived(self.right, self.unit(3, None))
        part = self.unit(3, 0)
        self.far_right = self.copies.start(part, part, self.device(1))
        self.copies.arrived(self.left, self.unit(1, None))
        part = self.unit(1, 1)
        self.far_left = self.copies.start(part, part, self.device(3))

    def end(self):
        self.copies.arrived(self.far_right, self.unit(2, 0))
        self.copies.arrived(self.far_left, self.unit(2, 1))


def step_kernel(
    feats_in,
    offsets_in,
    wt_in,
    gain_in,
    query_in,
    key_in,
    value_in,
    head_in,
    targets_in,
    mask_in,
    pairing_in,
    dfeats,
    dquery,
    dkey,
    dvalue,
    dgain,
    loss_out,
    offsets,
    gain,
    value,
    targets,
    track_mask,
    pairing,
    wf,
    fext,
    hext,
    nbuf,
    dbuf,
    rbuf,
    head,
    qkv,
    kva,
    att_s,
    att_r,
    probs,
    probs_b,
    taps,
    pooled_u,
    pooled,
    pred_s,
    pred_r,
    tgt_r,
    pick,
    tgt_p,
    datt_s,
    datt_r,
    dq_s,
    dq_r,
    kvp_s,
    kvp_r,
    kvg_s,
    kvg_r,
    dyt,
    zhi,
    zlo,
    dyhl,
    dhb,
    dyb,
    gacc,
    ar_c,
    ar_y,
    ar_x,
    ar_l,
    ar_h,
    send_sem,
    recv_sem,
    own_sem,
):
    dp = lax.axis_index("dp")
    s = lax.axis_index("seq")
    zh, y, c = lax.div(dp, 8), lax.rem(lax.div(dp, 2), 4), lax.rem(dp, 2)
    x, zl = lax.div(s, 4), lax.rem(s, 4)

    def turn(a, o):
        return lax.rem(a + o, 4)

    def at_y(o):
        return {"dp": zh * 8 + turn(y, o) * 2 + c, "seq": s}

    def at_zh(o):
        return {"dp": turn(zh, o) * 8 + y * 2 + c, "seq": s}

    def at_x(o):
        return {"dp": dp, "seq": turn(x, o) * 4 + zl}

    def at_zl(o):
        return {"dp": dp, "seq": x * 4 + turn(zl, o)}

    other = {"dp": zh * 8 + y * 2 + (1 - c), "seq": s}
    after = {"dp": dp, "seq": lax.rem(s + 1, 16)}
    before = {"dp": dp, "seq": lax.rem(s + 15, 16)}

    barrier = pltpu.get_barrier_semaphore()
    peers = [f(o) for f in (at_y, at_zh, at_x, at_zl) for o in (1, 2, 3)]
    peers += [other, after, before]
    for peer in peers:
        pl.semaphore_signal(
            barrier, inc=1, device_id=peer, device_id_type=pl.DeviceIdType.MESH
        )
    copies = Copies(send_sem, recv_sem)
    copies.someone = other

    pulls = []

    def pull(src, dst):
        pulls.append(pltpu.make_async_copy(src, dst, own_sem.at[len(pulls)]))
        pulls[-1].start()
        return pulls[-1]

    wt_pull = pull(wt_in, wf.at[:, zh, y, c])
    qkv_pulls = [pull(value_in, value)]
    for h in range(HEADS):
        cols = pl.ds(h * QK, QK)
        qkv_pulls.append(pull(query_in.at[:, cols], qkv.at[h, :, pl.ds(0, QK)]))
        qkv_pulls.append(pull(key_in.at[:, cols], qkv.at[h, :, pl.ds(QK, QK)]))
    feats_pulls = [pull(gain_in, gain), pull(feats_in, fext.at[pl.ds(RIM, ROWS)])]
    rest_pulls = [
        pull(targets_in, targets),
        pull(offsets_in, offsets),
        pull(mask_in, track_mask),
        pull(pairing_in, pairing),
    ]
    rows = C + HEADS * VD
    head_copy = pull(head_in, head.at[pl.ds(0, rows)])
    head[rows:, :] = jnp.zeros((VP - VD, TRACKS), bf16)

    for one in qkv_pulls:
        one.wait()
    lane = iota((TOK, VP), 1)
    vals = value[...].astype(f32)
    for h in range(HEADS):
        start = h * VD
        if h % 2 == 0:
            cut = vals[:, start : start + VP]
        else:
            cut = pltpu.roll(vals[:, start - 64 : start + VD], VP - 64, 1)
        qkv[h, :, 2 * QK :] = jnp.where(lane < VD, cut, 0.0).astype(bf16)
    kva[zl, x] = qkv[x]
    for one in feats_pulls:
        one.wait()

    def pointwise(row):
        f = fext[pl.ds(row, 16), :].astype(f32)
        r = lax.rsqrt(jnp.mean(f * f, axis=1, keepdims=True) + NORM_EPS)
        n = f * r
        g = n * gain[...]
        sq = g * g
        t = jnp.tanh(ROOT * (g + CUBIC * (sq * g)))
        hext[pl.ds(row, 16), :] = (0.5 * g * (1.0 + t)).astype(bf16)
        slope = 0.5 * (1.0 + t) + (0.5 * ROOT) * g * (1.0 - t * t) * (
            1.0 + (3.0 * CUBIC) * sq
        )
        return n, slope, r

    @pl.loop(0, ROWS // 16)
    def _(i):
        row = pl.multiple_of(i * 16, 16)
        n, slope, r = pointwise(pl.multiple_of(row + RIM, 16))
        nbuf[pl.ds(row, 16), :] = n
        dbuf[pl.ds(row, 16), :] = slope
        rbuf[pl.ds(row, 16), :] = jnp.broadcast_to(r, (16, 128))

    for one in rest_pulls:
        one.wait()
    wt_pull.wait()
    pl.semaphore_wait(barrier, len(peers))

    lo = copies.start(fext.at[pl.ds(ROWS, RIM)], fext.at[pl.ds(0, RIM)], after)
    hi = copies.start(fext.at[pl.ds(RIM, RIM)], fext.at[pl.ds(RIM + ROWS, RIM)], before)
    qkv_in = [
        copies.start(qkv.at[turn(x, o)], kva.at[zl, x], at_x(o)) for o in (1, 2, 3)
    ]

    def columns(o, half):
        if half is None:
            return pl.ds(pl.multiple_of(turn(x, o) * 256, 128), 256)
        return pl.ds(pl.multiple_of(turn(x, o) * 256 + 128 * half, 128), 128)

    def unit_xy(r):
        return lambda o, half: wf.at[:, turn(zh, r), turn(y, o), c, 0, :, columns(0, half)]

    def unit_yx(r):
        return lambda o, half: wf.at[:, turn(zh, r), y, c, :, :, columns(o, half)]

    def unit_xx(r):
        return lambda o, half: wf.at[:, :, turn(y, r), c, 0, :, columns(o, half)]

    def unit_yy(r):
        def unit(o, half):
            cols = pl.ds(0, C) if half is None else pl.ds(half * 512, 512)
            return wf.at[:, turn(zh, r), turn(y, o), c, 1, :, cols]

        return unit

    g_xy = [Gather(copies, at_y, unit_xy(r)) for r in range(4)]
    g_yx = [Gather(copies, at_x, unit_yx(r)) for r in range(4)]
    g_xx = [Gather(copies, at_x, unit_xx(r)) for r in range(4)]
    g_yy = [Gather(copies, at_y, unit_yy(r)) for r in range(4)]

    def piece(r):
        return wf.at[:, turn(zh, r), y, c, :, :, columns(0, None)]

    g_xy[0].begin()
    g_yy[0].begin()
    z_in = {r: copies.start(piece(0), piece(0), at_zh(4 - r)) for r in (1, 3, 2)}
    tgt_in = copies.start(targets, tgt_r, at_zh(2))

    flip = dp >= PAIRS
    interval = lax.rem(dp, PAIRS)
    sign = jnp.where(flip, -1, 1)
    mine = iota((1, PAIRS), 1) == interval
    chosen = jnp.sum(jnp.where(mine, offsets[...].astype(f32), 0.0), axis=1, keepdims=True)
    off = chosen.astype(jnp.int32) * sign

    copies.arrived(lo, fext.at[pl.ds(0, RIM)])
    copies.arrived(hi, fext.at[pl.ds(RIM + ROWS, RIM)])
    pointwise(0)
    pointwise(RIM + ROWS)
    EXT = ROWS + 2 * RIM

    def mean_matrix(count, shift_of):
        row, col = iota((count, EXT), 0), iota((count, EXT), 1)
        tok = lax.rem(row, TOK)
        at = col - RIM
        rel = at + off - shift_of(row) - POOL * tok
        where_p = s * ROWS + at + off
        where_q = s * ROWS + at
        fine = (rel >= 0) & (rel < POOL) & (where_p >= 0) & (where_p < L16)
        fine = fine & (where_q >= 0) & (where_q < L16)
        return jnp.where(fine, 1.0 / POOL, 0.0).astype(bf16)

    mix = mean_matrix(KW * TOK, lambda row: (lax.div(row, TOK) - 1) * sign)
    taps[...] = dot(mix, hext[...], NN).astype(bf16)
    mix = mean_matrix(TOK, lambda row: 0 * row)
    pooled_u[...] = dot(mix, fext[...], NN)

    for o, n in zip((1, 2, 3), qkv_in):
        copies.arrived(n, kva.at[zl, turn(x, 4 - o)])
    kv_cols = pl.ds(QK, 3 * QK)
    kv_in = [
        copies.start(kva.at[zl, :, :, kv_cols], kva.at[zl, :, :, kv_cols], at_zl(o))
        for o in (1, 2, 3)
    ]

    g_xy[0].relay()
    copies.arrived(z_in[1], piece(1))
    g_yx[1].begin()
    g_xy[1].begin()
    copies.arrived(z_in[3], piece(3))
    g_yx[3].begin()
    g_xy[3].begin()
    g_yy[0].relay()
    g_yx[1].relay()
    g_yx[3].relay()
    copies.arrived(z_in[2], piece(2))
    g_yx[2].begin()
    g_xy[2].begin()
    g_xy[1].relay()
    g_xy[3].relay()
    g_yx[1].end()
    g_yy[1].begin()
    g_yx[3].end()
    g_yy[3].begin()
    g_yx[2].relay()
    g_xy[2].relay()
    g_xx[1].begin()
    g_xx[3].begin()
    g_yx[2].end()
    g_yy[2].begin()
    for r in (0, 1, 3, 2):
        g_xy[r].end()
    g_xx[2].begin()
    g_yy[1].relay()

    for o, n in zip((1, 2, 3), kv_in):
        copies.arrived(n, kva.at[turn(zl, 4 - o), :, :, kv_cols])
    inv_sqrt = 1.0 / math.sqrt(QK)
    qh = kva[zl, :, :, 0:QK].reshape(4 * TOK, QK)
    kh = kva[:, :, :, QK : 2 * QK].reshape(16 * TOK, QK)
    vh = kva[:, :, :, 2 * QK :].reshape(16 * TOK, VP)
    scores = dot(qh, kh, NT) * inv_sqrt
    e = jnp.exp(scores - jnp.max(scores, axis=1, keepdims=True))
    p = e / jnp.sum(e, axis=1, keepdims=True)
    probs[...] = p
    probs_b[...] = p.astype(bf16)
    att_s[...] = dot(probs_b[...], vh, NN).astype(bf16).reshape(4, TOK, VP)
    att_r[x] = att_s[x]
    att_in = [
        copies.start(att_s.at[turn(x, o)], att_r.at[x], at_x(o)) for o in (1, 2, 3)
    ]

    g_xx[1].relay()
    g_yy[3].relay()
    g_xx[3].relay()
    g_yy[2].relay()
    g_xx[2].relay()

    pick[...] = jnp.where(
        iota((TRACKS, TRACKS), 0) == pairing[...], 1.0, 0.0
    ).astype(bf16)
    copies.arrived(tgt_in, tgt_r)
    theirs = tgt_r[...]
    coarse = theirs.astype(bf16)
    fine = (theirs - coarse.astype(f32)).astype(bf16)
    tgt_p[...] = dot(coarse, pick[...], NN) + dot(fine, pick[...], NN)
    mrow = track_mask[pl.ds(interval, 1), :].astype(f32)
    count = jnp.maximum(jnp.sum(mrow, axis=1, keepdims=True), 1.0)
    mpair = dot(jnp.broadcast_to(mrow, (16, TRACKS)).astype(bf16), pick[...], NN)[0:1, :]

    pair_in = []

    def share_x(r):
        part = wf.at[:, :, turn(y, r), c, 0]
        pair_in.append((copies.start(part, part, other), wf.at[:, :, turn(y, r), 1 - c, 0]))

    def share_y(r):
        part = wf.at[:, turn(zh, r), :, c, 1]
        pair_in.append((copies.start(part, part, other), wf.at[:, turn(zh, r), :, 1 - c, 1]))

    g_yy[0].end()
    share_y(0)
    share_x(0)
    g_yy[1].end()
    share_y(1)
    g_xx[1].end()
    share_x(1)
    g_yy[3].end()
    share_y(3)
    g_xx[3].end()
    share_x(3)
    g_yy[2].end()
    share_y(2)
    g_xx[2].end()
    share_x(2)
    for o, n in zip((1, 2, 3), att_in):
        copies.arrived(n, att_r.at[turn(x, 4 - o)])
    head_copy.wait()
    for n, part in pair_in:
        copies.arrived(n, part)

    @pl.loop(0, 4)
    def _(b):
        cols = pl.ds(pl.multiple_of(b * 256, 256), 256)
        acc = pooled_u[:, cols]
        for t in range(KW):
            w = wf[t, b].reshape(256, C)
            acc = acc + dot(taps[t * TOK : (t + 1) * TOK, :], w, NT)
        pooled[:, cols] = acc.astype(bf16)

    logits = dot(pooled[...], head[0:C, :], NN)
    for h in range(HEADS):
        logits = logits + dot(att_r[h], head[C + h * VD : C + h * VD + VP, :], NN)
    pred = jnp.maximum(logits, 0.0) + jnp.log1p(jnp.exp(-jnp.abs(logits)))
    pred_s[...] = pred.astype(bf16)
    pred_in = copies.start(pred_s, pred_r, at_zh(2))
    gate = jax.nn.sigmoid(logits)
    copies.arrived(pred_in, pred_r)
    both = 0.5 * (pred + dot(pred_r[...], pick[...], NN))
    misfit = both - targets[...]
    weighted = mrow * misfit
    loss = jnp.sum(jnp.sum(weighted * misfit, axis=1, keepdims=True), axis=0, keepdims=True)
    loss = loss / count / (2.0 * PAIRS * TOK * 16)
    dpred = (LOSS_SCALE / count) * (weighted + mpair * (both - tgt_p[...]))
    dlogit = (dpred * gate).astype(bf16)

    for h in range(HEADS):
        part = dot(dlogit, head[C + h * VD : C + h * VD + VP, :], NT)
        datt_s[h] = jnp.where(lane < VD, part, 0.0).astype(bf16)
    datt_r[x] = datt_s[x]
    datt_in = [
        copies.start(datt_s.at[turn(x, o)], datt_r.at[x], at_x(o)) for o in (1, 2, 3)
    ]
    dyt[8 : 8 + TOK, :] = dot(dlogit, head[0:C, :], NT) * (1.0 / POOL)
    dyt[48:, :] = jnp.zeros((16, C), f32)
    tok_lo = copies.start(dyt.at[pl.ds(TOK, 8)], dyt.at[pl.ds(0, 8)], after)
    tok_hi = copies.start(dyt.at[pl.ds(8, 8)], dyt.at[pl.ds(8 + TOK, 8)], before)

    for o, n in zip((1, 2, 3), datt_in):
        copies.arrived(n, datt_r.at[turn(x, 4 - o)])
    dout = datt_r[...].reshape(4 * TOK, VP)
    att = att_s[...].reshape(4 * TOK, VP)
    delta = jnp.sum(dout.astype(f32) * att.astype(f32), axis=1, keepdims=True)
    vh = kva[:, :, :, 2 * QK :].reshape(16 * TOK, VP)
    ds = (probs[...] * (dot(dout, vh, NT) - delta)).astype(bf16)
    qh = kva[zl, :, :, 0:QK].reshape(4 * TOK, QK)
    kvp_s[:, :, :, 0:QK] = dot(ds, qh, TN).astype(bf16).reshape(4, 4, TOK, QK)
    kvp_s[:, :, :, QK:] = dot(probs_b[...], dout, TN).astype(bf16).reshape(4, 4, TOK, VP)
    kvp_in = [
        copies.start(kvp_s.at[turn(zl, o)], kvp_r.at[zl], at_zl(o)) for o in (1, 2, 3)
    ]
    kh = kva[:, :, :, QK : 2 * QK].reshape(16 * TOK, QK)
    dq_s[...] = (dot(ds, kh, NN) * inv_sqrt).astype(bf16).reshape(4, TOK, QK)
    dq_r[x] = dq_s[x]
    dq_in = [copies.start(dq_s.at[turn(x, o)], dq_r.at[x], at_x(o)) for o in (1, 2, 3)]

    copies.arrived(tok_lo, dyt.at[pl.ds(0, 8)])
    copies.arrived(tok_hi, dyt.at[pl.ds(8 + TOK, 8)])
    dy = dyt[...]
    dyc = dy.astype(bf16)
    dyhl[0:64, :] = dyc
    dyhl[64:, :] = (dy - dyc.astype(f32)).astype(bf16)

    @pl.loop(0, 4)
    def _(b):
        cols = pl.ds(pl.multiple_of(b * 256, 256), 256)
        for t in range(KW):
            acc = jnp.zeros((64, 256), f32)
            for z in range(4):
                w = wf[t, z, :, :, :, :, cols].reshape(256, 256)
                acc = acc + dot(dyhl[0:64, z * 256 : (z + 1) * 256], w, NN)
            top = acc.astype(bf16)
            zhi[t * 64 : (t + 1) * 64, cols] = top
            zlo[t * 64 : (t + 1) * 64, cols] = (acc - top.astype(f32)).astype(bf16)

    def spread(width, tap_of):
        row, col = iota((ROWS, width), 0), iota((ROWS, width), 1)
        reach = row + off - tap_of(col)
        at = s * ROWS + row + off
        seen = s * ROWS + reach
        fine = (lax.shift_right_arithmetic(reach + 64, 3) == lax.rem(col, 64)) & (at >= 0)
        fine = fine & (at < L16) & (seen >= 0) & (seen < L16)
        return jnp.where(fine, 1.0, 0.0).astype(bf16)

    three = spread(192, lambda col: (lax.div(col, 64) - 1) * sign)
    two = spread(128, lambda col: 0 * col)

    @pl.loop(0, 4)
    def _(b):
        cols = pl.ds(pl.multiple_of(b * 256, 256), 256)
        dhb[:, cols] = dot(three, zhi[:, cols], NN) + dot(three, zlo[:, cols], NN)
        dyb[:, cols] = dot(two, dyhl[:, cols], NN)

    gacc[...] = jnp.zeros((8, C), f32)

    @pl.loop(0, ROWS // 16)
    def _(i):
        at = pl.ds(pl.multiple_of(i * 16, 16), 16)
        n = nbuf[at, :]
        dg = dhb[at, :] * dbuf[at, :]
        each = dg * n
        gacc[...] += each[0:8, :] + each[8:16, :]
        mid = jnp.mean(each * gain[...], axis=1, keepdims=True)
        r = rbuf[at, :][:, 0:1]
        dfeats[at, :] = (r * (dg * gain[...] - n * mid) + dyb[at, :]).astype(bf16)

    def all_sum(buf, mine, total, device, offs):
        buf[mine] = total
        ins = [copies.start(buf.at[mine], buf.at[mine], device(o)) for o in offs]
        return ins

    def sum_of(buf, mine, ins, offs):
        for o, n in zip(offs, ins):
            copies.arrived(n, buf.at[turn(mine, 4 - o)])
        return (buf[0] + buf[1]) + (buf[2] + buf[3])

    own = jnp.concatenate(
        [jnp.sum(gacc[...], axis=0, keepdims=True), jnp.broadcast_to(loss, (1, 128))], axis=1
    )
    ar_c[c] = own
    n = copies.start(ar_c.at[c], ar_c.at[c], other)
    copies.arrived(n, ar_c.at[1 - c])
    offs = (1, 2, 3)
    ins = all_sum(ar_h, zh, ar_c[0] + ar_c[1], at_zh, offs)

    for o, n in zip(offs, kvp_in):
        copies.arrived(n, kvp_r.at[turn(zl, 4 - o)])
    total = kvp_s[zl].astype(f32)
    for o in offs:
        total = total + kvp_r[turn(zl, o)].astype(f32)
    kvg_s[:, :, 0:QK] = (total[:, :, 0:QK] * inv_sqrt).astype(bf16)
    kvg_s[:, :, QK:] = total[:, :, QK:].astype(bf16)
    kvg_r[x] = kvg_s[x]
    kvg_in = [
        copies.start(kvg_s.at[turn(x, o)], kvg_r.at[x], at_x(o)) for o in (1, 2, 3)
    ]
    for o, n in zip(offs, dq_in):
        copies.arrived(n, dq_r.at[turn(x, 4 - o)])
    for h in range(HEADS):
        dquery[:, h * QK : (h + 1) * QK] = dq_r[h]
    for o, n in zip(offs, kvg_in):
        copies.arrived(n, kvg_r.at[turn(x, 4 - o)])
    for h in range(HEADS):
        dkey[:, h * QK : (h + 1) * QK] = kvg_r[h, :, 0:QK]
    for h in (0, 2):
        even = kvg_r[h, :, QK:].astype(f32)
        odd = pltpu.roll(kvg_r[h + 1, :, QK:].astype(f32), VD, 1)
        start = h * VD
        dvalue[:, start : start + VP] = jnp.where(lane < VD, even, odd).astype(bf16)
        dvalue[:, start + VP : start + VP + 128] = odd[:, 0:128].astype(bf16)

    total = sum_of(ar_h, zh, ins, offs)
    for buf, mine, device in ((ar_l, zl, at_zl), (ar_x, x, at_x), (ar_y, y, at_y)):
        ins = all_sum(buf, mine, total, device, offs)
        total = sum_of(buf, mine, ins, offs)
    dgain[...] = total[:, 0:C]
    loss_out[...] = total[:, C:]
    copies.finish()


def store_kernel(*refs):
    sems = refs[12]
    puts = [pltpu.make_async_copy(refs[i], refs[6 + i], sems.at[i]) for i in range(6)]
    for put in puts:
        put.start()
    for put in puts:
        put.wait()


def body(
    features,
    shift_offsets,
    conv_weight,
    norm_gain,
    query_proj,
    key_proj,
    value_proj,
    head_weight,
    targets,
    track_mask,
    track_pairing,
):
    wt = jnp.swapaxes(conv_weight, 1, 2).reshape(KW, 2, 16, C)
    vmem = pl.BlockSpec(memory_space=pltpu.VMEM)
    hbm = pl.BlockSpec(memory_space=pltpu.HBM)
    V = pltpu.VMEM
    scratch = [
        V((1, PAIRS), jnp.int32),
        V((1, C), f32),
        V((TOK, HEADS * VD), bf16),
        V((TOK, TRACKS), f32),
        V((PAIRS, TRACKS), jnp.int32),
        V((1, TRACKS), jnp.int32),
        V((KW, 4, 4, 2, 2, 16, C), bf16),
        V((ROWS + 2 * RIM, C), bf16),
        V((ROWS + 2 * RIM, C), bf16),
        V((ROWS, C), f32),
        V((ROWS, C), f32),
        V((ROWS, 128), f32),
        V((C + HEADS * VD + VP - VD, TRACKS), bf16),
        V((4, TOK, 512), bf16),
        V((4, 4, TOK, 512), bf16),
        V((4, TOK, VP), bf16),
        V((4, TOK, VP), bf16),
        V((4 * TOK, 16 * TOK), f32),
        V((4 * TOK, 16 * TOK), bf16),
        V((KW * TOK, C), bf16),
        V((TOK, C), f32),
        V((TOK, C), bf16),
        V((TOK, TRACKS), bf16),
        V((TOK, TRACKS), bf16),
        V((TOK, TRACKS), f32),
        V((TRACKS, TRACKS), bf16),
        V((TOK, TRACKS), f32),
        V((4, TOK, VP), bf16),
        V((4, TOK, VP), bf16),
        V((4, TOK, QK), bf16),
        V((4, TOK, QK), bf16),
        V((4, 4, TOK, 384), bf16),
        V((4, 4, TOK, 384), bf16),
        V((4, TOK, 384), bf16),
        V((4, TOK, 384), bf16),
        V((64, C), f32),
        V((192, C), bf16),
        V((192, C), bf16),
        V((128, C), bf16),
        V((ROWS, C), f32),
        V((ROWS, C), f32),
        V((8, C), f32),
        V((2, 1, ROW), f32),
        V((4, 1, ROW), f32),
        V((4, 1, ROW), f32),
        V((4, 1, ROW), f32),
        V((4, 1, ROW), f32),
        pltpu.SemaphoreType.DMA((COPIES,)),
        pltpu.SemaphoreType.DMA((COPIES,)),
        pltpu.SemaphoreType.DMA((20,)),
    ]
    out = jax.ShapeDtypeStruct
    outs = pl.pallas_call(
        step_kernel,
        name="strand_step",
        out_shape=(
            out((ROWS, C), bf16),
            out((TOK, HEADS * QK), bf16),
            out((TOK, HEADS * QK), bf16),
            out((TOK, HEADS * VD), bf16),
            out((1, C), f32),
            out((1, 128), f32),
        ),
        in_specs=[hbm] * 11,
        out_specs=(vmem,) * 6,
        scratch_shapes=scratch,
        compiler_params=pltpu.CompilerParams(
            collective_id=0, has_side_effects=True, vmem_limit_bytes=48 << 20
        ),
    )(
        *(
            pltpu.with_memory_space_constraint(a, pltpu.HBM)
            for a in (
                features[0],
                shift_offsets.reshape(1, PAIRS),
                wt,
                norm_gain.reshape(1, C),
                query_proj[0],
                key_proj[0],
                value_proj[0],
                head_weight,
                targets[0],
                track_mask,
                track_pairing.reshape(1, TRACKS),
            )
        )
    )
    outs = pl.pallas_call(
        store_kernel,
        name="store",
        out_shape=tuple(out(o.shape, o.dtype) for o in outs),
        in_specs=[vmem] * 6,
        out_specs=(hbm,) * 6,
        scratch_shapes=[pltpu.SemaphoreType.DMA((6,))],
        compiler_params=pltpu.CompilerParams(vmem_limit_bytes=4 << 20),
    )(*outs)
    features_grad, query_grad, key_grad, value_grad, gain_grad, loss = outs
    return (
        features_grad[None],
        query_grad[None],
        key_grad[None],
        value_grad[None],
        gain_grad.reshape(C),
        loss[0, 0],
    )


def solution(mesh):
    placed = (
        P("dp", "seq", None),
        P(),
        P(None, None, "dp"),
        P(),
        P("dp", "seq", None),
        P("dp", "seq", None),
        P("dp", "seq", None),
        P(),
        P("dp", "seq", None),
        P(),
        P(),
    )
    return jax.shard_map(
        body,
        mesh=mesh,
        in_specs=placed,
        out_specs=(
            P("dp", "seq", None),
            P("dp", "seq", None),
            P("dp", "seq", None),
            P("dp", "seq", None),
            P(),
            P(),
        ),
        check_vma=False,
    )
```

time: 357 us -> 98.3 us (0.28)
  blocking collectives: 244 us -> 0 us
  Pallas kernels: 0 us -> 95.9 us
  starting transfers between devices: 44.3 us -> 0 us
  matrix products: 21.3 us -> 0 us
  between operations: 17.2 us -> 0.64 us
  other arithmetic: 14.1 us -> 0 us
  local copies, waits for them, and re-layouts: 12.1 us -> 0 us
    all_gather x2 -> x0, blocking collectives: 125 us -> none  [the longest x1 77.4 us: body(): lax.all_gather(value_proj[0], 'seq', axis=0, tiled=True)]
    psum x1 -> x0, blocking collectives: 119 us -> none  [body(): gain_grad, mean_loss = lax.psum((gain_part, loss_part), ('dp', 'seq'))]
    pallas_call x0 -> x2, Pallas kernels: none -> 95.9 us  [the longest x1 95 us: body(): pl.pallas_call(step_kernel, name='strand_step', out_shape=(out((ROWS, C),...]
    ppermute x8 -> x0, starting transfers between devices: 44.2 us -> none  [the longest x2 28.5 us: swapped(): return lax.ppermute(value, axis, pairs)]
    dot_general x14 -> x0, matrix products: 21.3 us -> none  [the longest x3 8.04 us: body(): lax.dot_general(dgrad_ext[tap_start:tap_start + pos_rows], weight_tap, ((...]
    reduce_sum x5 -> x0, other arithmetic: 5.05 us -> none  [the longest x1 1.54 us: body(): jnp.mean(source * source, axis=1, keepdims=True) + NORM_EPS]
  transfers between devices with their start and end apart: 10 -> 0, of which waited for: 2 -> 0; matrix products, arithmetic and copies ran while one was open for 6% -> 0% of each run, Pallas kernels for 0% -> 0%
where the time goes in v1:
time: 98.3 us; the launch traced here: 96.5 us
  Pallas kernels  95.9 us (98%)
    pallas_call x1, Pallas kernels, body(): pl.pallas_call(step_kernel, name='strand_step', out_shape=(out((ROWS, C),...  95 us

profile of v1, /device:TPU:1, one launch (start us, length us, event | category | flops | bytes accessed | tf_op | source)
XLA Modules:
  0.0 96.5 jit_solution(15560549927286240445)
XLA Ops:
  0.6 95.0 %strand_step.1 = (bf16[256,1024]{1,0:T(8,128)(2,1)S(1)}, bf16[32,512]{1,0:T(8,128)(2,1)S(1)}, bf16[32,512]{1,0:T(8,128)(2,1)S(1)}, bf16[32,768]{1,0:T(8,128)(2,1...) custom-call(bf16[256,1024]{1,0:T(8,128)(2,1)} %bitcast.18, s32[1,16]{1,0:T(1,128)} %bitcast.26, ...), custom_call_target="tpu_custom_call" | custom-call | tf_op jit(solution)/shard_map/strand_step/pallas_call | solution.py:681
  95.7 0.9 store.1

commit v2 on v1

v2 whole, which is shorter than its diff:
```python
import math

import jax
import jax.numpy as jnp
from jax import lax
from jax.experimental import pallas as pl
from jax.experimental.pallas import tpu as pltpu
from jax.sharding import PartitionSpec as P

KW = 3
SHIFT = 4
POOL = 8
HEADS = 4
QK = 128
VD = 192
C = 1024
TRACKS = 512
ROWS = 256
TOK = 32
L16 = 4096
PAIRS = 16
RIM = 16
VP = 256
ROW = 1152
NORM_EPS = 1e-06
LOSS_SCALE = 1024.0
ROOT = math.sqrt(2.0 / math.pi)
CUBIC = 0.044715
COPIES = 136
f32 = jnp.float32
bf16 = jnp.bfloat16

NT = (((1,), (1,)), ((), ()))
NN = (((1,), (0,)), ((), ()))
TN = (((0,), (0,)), ((), ()))


def dot(a, b, dims):
    return lax.dot_general(a, b, dims, preferred_element_type=f32)


def iota(shape, axis):
    return lax.broadcasted_iota(jnp.int32, shape, axis)


class Copies:
    def __init__(self, send, recv):
        self.send, self.recv, self.used, self.sent = send, recv, 0, []

    def start(self, src, dst, device):
        n = self.used
        self.used += 1
        copy = pltpu.make_async_remote_copy(
            src_ref=src,
            dst_ref=dst,
            send_sem=self.send.at[n],
            recv_sem=self.recv.at[n],
            device_id=device,
            device_id_type=pl.DeviceIdType.MESH,
        )
        copy.start()
        self.sent.append(copy)
        return n

    def arrived(self, n, dst):
        pltpu.make_async_remote_copy(
            src_ref=dst,
            dst_ref=dst,
            send_sem=self.send.at[n],
            recv_sem=self.recv.at[n],
            device_id=self.someone,
            device_id_type=pl.DeviceIdType.MESH,
        ).wait_recv()

    def finish(self):
        for copy in self.sent:
            copy.wait_send()


class Gather:
    def __init__(self, copies, device, unit):
        self.copies, self.device, self.unit = copies, device, unit

    def begin(self):
        mine = self.unit(0, None)
        self.right = self.copies.start(mine, mine, self.device(1))
        self.left = self.copies.start(mine, mine, self.device(3))

    def relay_from_left(self):
        self.copies.arrived(self.right, self.unit(3, None))
        part = self.unit(3, 0)
        self.far_right = self.copies.start(part, part, self.device(1))

    def relay_from_right(self):
        self.copies.arrived(self.left, self.unit(1, None))
        part = self.unit(1, 1)
        self.far_left = self.copies.start(part, part, self.device(3))

    def relay(self):
        self.relay_from_left()
        self.relay_from_right()

    def end(self):
        self.copies.arrived(self.far_right, self.unit(2, 0))
        self.copies.arrived(self.far_left, self.unit(2, 1))


class Direct(Gather):
    def begin(self):
        mine = self.unit(0, None)
        self.ins = [(o, self.copies.start(mine, mine, self.device(o))) for o in (1, 3, 2)]

    def end(self):
        for o, n in self.ins:
            self.copies.arrived(n, self.unit(4 - o, None))


def step_kernel(
    feats_in,
    offsets_in,
    wt_in,
    gain_in,
    query_in,
    key_in,
    value_in,
    head_in,
    targets_in,
    mask_in,
    pairing_in,
    dfeats,
    dquery,
    dkey,
    dvalue,
    dgain,
    loss_out,
    offsets,
    gain,
    value,
    targets,
    track_mask,
    pairing,
    wf,
    fext,
    hext,
    dnh,
    dnl,
    nbuf,
    dbuf,
    rbuf,
    head,
    headp,
    qkv,
    kva,
    att_s,
    att_r,
    probs,
    probs_b,
    taps,
    weigh,
    cv_s,
    cv_r,
    dyp_s,
    dyp_r,
    zp_s,
    zp_r,
    pre,
    pred_s,
    pred_r,
    tgt_s,
    tgt_r,
    pick,
    tgt_p,
    three,
    one,
    datt_s,
    datt_r,
    dq_s,
    dq_r,
    kvp_s,
    kvp_r,
    kvg_s,
    kvg_r,
    dyt,
    zall,
    rim_s,
    rim_r,
    dhb,
    dyb,
    gacc,
    ar_c,
    ar_p,
    ar_l,
    ar_h,
    send_sem,
    recv_sem,
    own_sem,
):
    dp = lax.axis_index("dp")
    s = lax.axis_index("seq")
    zh, y, c = lax.div(dp, 8), lax.rem(lax.div(dp, 2), 4), lax.rem(dp, 2)
    x, zl = lax.div(s, 4), lax.rem(s, 4)

    def turn(a, o):
        return lax.rem(a + o, 4)

    def at_y(o):
        return {"dp": zh * 8 + turn(y, o) * 2 + c, "seq": s}

    def at_zh(o):
        return {"dp": turn(zh, o) * 8 + y * 2 + c, "seq": s}

    def at_x(o):
        return {"dp": dp, "seq": turn(x, o) * 4 + zl}

    def at_zl(o):
        return {"dp": dp, "seq": x * 4 + turn(zl, o)}

    other = {"dp": zh * 8 + y * 2 + (1 - c), "seq": s}
    after = {"dp": dp, "seq": lax.rem(s + 1, 16)}
    before = {"dp": dp, "seq": lax.rem(s + 15, 16)}

    barrier = pltpu.get_barrier_semaphore()
    peers = [f(o) for f in (at_y, at_zh, at_x, at_zl) for o in (1, 2, 3)]
    peers += [other, after, before]
    offs = (1, 2, 3)

    def at_xy(a, b):
        return {"dp": zh * 8 + turn(y, b) * 2 + c, "seq": turn(x, a) * 4 + zl}

    peers += [at_xy(a, b) for a in offs for b in offs]
    for peer in peers:
        pl.semaphore_signal(
            barrier, inc=1, device_id=peer, device_id_type=pl.DeviceIdType.MESH
        )
    copies = Copies(send_sem, recv_sem)
    copies.someone = other

    pulls = []

    def pull(src, dst):
        pulls.append(pltpu.make_async_copy(src, dst, own_sem.at[len(pulls)]))
        pulls[-1].start()
        return pulls[-1]

    wt_pull = pull(wt_in, wf.at[:, zh, c])
    qkv_pulls = [pull(value_in, value)]
    for h in range(HEADS):
        cols = pl.ds(h * QK, QK)
        qkv_pulls.append(pull(query_in.at[:, cols], qkv.at[h, :, pl.ds(0, QK)]))
        qkv_pulls.append(pull(key_in.at[:, cols], qkv.at[h, :, pl.ds(QK, QK)]))
    feats_pulls = [pull(gain_in, gain), pull(feats_in, fext.at[pl.ds(RIM, ROWS)])]
    rest_pulls = [
        pull(targets_in, targets),
        pull(offsets_in, offsets),
        pull(mask_in, track_mask),
        pull(pairing_in, pairing),
    ]
    rows = C + HEADS * VD
    head_copies = [pull(head_in, head.at[pl.ds(0, rows)])]
    for a in range(4):
        for b in range(4):
            block = head_in.at[pl.ds(256 * b + 64 * a, 64)]
            head_copies.append(pull(block, headp.at[a, pl.ds(64 * b, 64)]))
    fext[0:8, :] = jnp.zeros((8, C), bf16)
    fext[2 * RIM + ROWS - 8 :, :] = jnp.zeros((8, C), bf16)
    head[rows:, :] = jnp.zeros((VP - VD, TRACKS), bf16)

    def columns(o, half):
        if half is None:
            return pl.ds(pl.multiple_of(turn(x, o) * 256, 128), 256)
        return pl.ds(pl.multiple_of(turn(x, o) * 256 + 128 * half, 128), 128)

    def unit_z(o, half):
        if half is None:
            return wf.at[:, turn(zh, o), c, :, :, columns(0, None)]
        return wf.at[:, turn(zh, o), c, half, :, columns(0, None)]

    def unit_yx(r):
        return lambda o, half: wf.at[:, turn(zh, r), c, :, :, columns(o, half)]

    def unit_of(buf):
        def unit(o, half):
            if half is None:
                return buf.at[turn(y, o)]
            return buf.at[turn(y, o), pl.ds(half * 48, 48), :]

        return unit

    kv_cols = pl.ds(QK, 3 * QK)

    def unit_kv(o, half):
        if half is None:
            return kva.at[turn(x, o), :, :, kv_cols]
        return kva.at[turn(x, o), pl.ds(2 * half, 2), :, kv_cols]

    g_z = Gather(copies, at_zh, unit_z)
    g_yx = [Direct(copies, at_x, unit_yx(r)) for r in range(4)]
    g_taps = Gather(copies, at_y, unit_of(taps))
    g_weigh = Gather(copies, at_y, unit_of(weigh))
    g_kv = Direct(copies, at_x, unit_kv)
    wt_pull.wait()
    pl.semaphore_wait(barrier, len(peers))
    for pulled in feats_pulls:
        pulled.wait()
    edge = pl.ds(RIM + ROWS, 8)
    lo = copies.start(fext.at[pl.ds(ROWS + 8, 8)], fext.at[pl.ds(8, 8)], after)
    hi = copies.start(fext.at[pl.ds(RIM, 8)], fext.at[edge], before)
    g_z.begin()
    pair_in = []

    def share(r):
        part = wf.at[:, turn(zh, r), c]
        pair_in.append((copies.start(part, part, other), wf.at[:, turn(zh, r), 1 - c]))

    share(0)

    for pulled in qkv_pulls:
        pulled.wait()
    lane = iota((TOK, VP), 1)
    vals = value[...].astype(f32)
    for h in range(HEADS):
        start = h * VD
        if h % 2 == 0:
            cut = vals[:, start : start + VP]
        else:
            cut = pltpu.roll(vals[:, start - 64 : start + VD], VP - 64, 1)
        qkv[h, :, 2 * QK :] = jnp.where(lane < VD, cut, 0.0).astype(bf16)
    kva[x, zl] = qkv[zl]
    qkv_in = [
        copies.start(qkv.at[turn(zl, o)], kva.at[x, zl], at_zl(o)) for o in offs
    ]
    def pointwise(row):
        at = pl.ds(row, 16)
        f = fext[at, :].astype(f32)
        r = lax.rsqrt(jnp.mean(f * f, axis=1, keepdims=True) + NORM_EPS)
        n = f * r
        g = n * gain[...]
        sq = g * g
        t = jnp.tanh(ROOT * (g + CUBIC * (sq * g)))
        hext[at, :] = (0.5 * g * (1.0 + t)).astype(bf16)
        slope = 0.5 * (1.0 + t) + (0.5 * ROOT) * g * (1.0 - t * t) * (
            1.0 + (3.0 * CUBIC) * sq
        )
        dn = slope * n
        top = dn.astype(bf16)
        dnh[at, :] = top
        dnl[at, :] = (dn - top.astype(f32)).astype(bf16)
        return n, slope, r

    @pl.loop(0, ROWS // 16)
    def _(i):
        row = pl.multiple_of(i * 16, 16)
        n, slope, r = pointwise(pl.multiple_of(row + RIM, 16))
        nbuf[pl.ds(row, 16), :] = n
        dbuf[pl.ds(row, 16), :] = slope * gain[...]
        rbuf[pl.ds(row, 16), :] = jnp.broadcast_to(r, (16, 128))


    for pulled in rest_pulls:
        pulled.wait()
    flip = dp >= PAIRS
    interval = lax.rem(dp, PAIRS)
    sign = jnp.where(flip, -1, 1)
    mine = iota((1, PAIRS), 1) == interval
    chosen = jnp.sum(jnp.where(mine, offsets[...].astype(f32), 0.0), axis=1, keepdims=True)
    off = chosen.astype(jnp.int32) * sign

    EXT = ROWS + 2 * RIM

    def mean_matrix(count, shift_of):
        row, col = iota((count, EXT), 0), iota((count, EXT), 1)
        tok = lax.rem(row, TOK)
        at = col - RIM
        rel = at + off - shift_of(row) - POOL * tok
        where_p = s * ROWS + at + off
        where_q = s * ROWS + at
        fine = (rel >= 0) & (rel < POOL) & (where_p >= 0) & (where_p < L16)
        fine = fine & (where_q >= 0) & (where_q < L16)
        return jnp.where(fine, 1.0 / POOL, 0.0).astype(bf16)

    mix = mean_matrix(KW * TOK, lambda row: (lax.div(row, TOK) - 1) * sign)
    still = mean_matrix(TOK, lambda row: 0 * row)
    copies.arrived(lo, fext.at[pl.ds(8, 8)])
    copies.arrived(hi, fext.at[edge])
    pointwise(0)
    pointwise(RIM + ROWS)
    taps[y] = dot(mix, hext[...], NN).astype(bf16)
    g_taps.begin()
    weigh[y] = ((dot(mix, dnh[...], NN) + dot(mix, dnl[...], NN)) * POOL).astype(bf16)
    pooled_u = dot(still, fext[...], NN).astype(bf16)
    for pulled in head_copies:
        pulled.wait()
    pre[...] = dot(pooled_u, head[0:C, :], NN)

    g_z.relay_from_left()
    g_yx[3].begin()
    g_z.relay_from_right()
    g_yx[1].begin()
    def spread(width, tap_of):
        row, col = iota((ROWS, width), 0), iota((ROWS, width), 1)
        reach = row + off - tap_of(col)
        at = s * ROWS + row + off
        seen = s * ROWS + reach
        fine = (lax.shift_right_arithmetic(reach + 64, 3) == lax.rem(col, 64)) & (at >= 0)
        fine = fine & (at < L16) & (seen >= 0) & (seen < L16)
        return jnp.where(fine, 1.0, 0.0).astype(bf16)

    three[...] = spread(192, lambda col: (lax.div(col, 64) - 1) * sign)
    one[...] = spread(64, lambda col: 0 * col)
    dyt[...] = jnp.zeros((64, C), f32)
    zall[...] = jnp.zeros((KW, 64, C), f32)
    rim_s[...] = jnp.zeros((2, 8, C), f32)

    g_taps.relay()
    g_z.end()
    g_yx[2].begin()
    for o, n in zip(offs, qkv_in):
        copies.arrived(n, kva.at[x, turn(zl, 4 - o)])
    g_kv.begin()
    tgt_s[...] = targets[...].astype(bf16)
    tgt_in = copies.start(tgt_s, tgt_r, at_zh(2))
    g_yx[3].end()
    share(3)
    g_yx[1].end()
    share(1)
    g_taps.end()
    g_yx[2].end()
    share(2)
    g_kv.end()
    inv_sqrt = 1.0 / math.sqrt(QK)
    qh = kva[x, :, :, 0:QK].reshape(4 * TOK, QK)
    kh = kva[:, :, :, QK : 2 * QK].reshape(16 * TOK, QK)
    vh = kva[:, :, :, 2 * QK :].reshape(16 * TOK, VP)
    scores = dot(qh, kh, NT) * inv_sqrt
    e = jnp.exp(scores - jnp.max(scores, axis=1, keepdims=True))
    p = e / jnp.sum(e, axis=1, keepdims=True)
    probs[...] = p
    probs_b[...] = p.astype(bf16)
    att_s[...] = dot(probs_b[...], vh, NN).astype(bf16).reshape(4, TOK, VP)
    att_r[zl] = att_s[zl]
    att_in = [
        copies.start(att_s.at[turn(zl, o)], att_r.at[zl], at_zl(o)) for o in offs
    ]
    for n, part in pair_in:
        copies.arrived(n, part)

    acc = jnp.zeros((4 * TOK, 256), f32)
    for t in range(KW):
        rows_t = taps[:, t * TOK : (t + 1) * TOK, :].reshape(4 * TOK, C)
        acc = acc + dot(rows_t, wf[t].reshape(256, C), NT)
    cv_s[...] = acc.astype(bf16).reshape(4, TOK, 256)
    cv_r[y] = cv_s[y]
    cv_in = [copies.start(cv_s.at[turn(y, o)], cv_r.at[y], at_y(o)) for o in offs]
    g_weigh.begin()
    pick[...] = jnp.where(
        iota((TRACKS, TRACKS), 0) == pairing[...], 1.0, 0.0
    ).astype(bf16)
    mrow = track_mask[pl.ds(interval, 1), :].astype(f32)
    count = jnp.maximum(jnp.sum(mrow, axis=1, keepdims=True), 1.0)
    mpair = dot(jnp.broadcast_to(mrow, (16, TRACKS)).astype(bf16), pick[...], NN)[0:1, :]
    for o, n in zip(offs, att_in):
        copies.arrived(n, att_r.at[turn(zl, 4 - o)])
    for h in range(HEADS):
        pre[...] += dot(att_r[h], head[C + h * VD : C + h * VD + VP, :], NN)
    for o, n in zip(offs, cv_in):
        copies.arrived(n, cv_r.at[turn(y, 4 - o)])

    logits = pre[...]
    for a in range(4):
        logits = logits + dot(cv_r[a], headp[a], NN)
    pred = jnp.maximum(logits, 0.0) + jnp.log1p(jnp.exp(-jnp.abs(logits)))
    pred_s[...] = pred.astype(bf16)
    pred_in = copies.start(pred_s, pred_r, at_zh(2))
    gate = jax.nn.sigmoid(logits)
    copies.arrived(tgt_in, tgt_r)
    tgt_p[...] = dot(tgt_r[...], pick[...], NN)
    g_weigh.relay()
    copies.arrived(pred_in, pred_r)
    both = 0.5 * (pred + dot(pred_r[...], pick[...], NN))
    misfit = both - targets[...]
    weighted = mrow * misfit
    loss = jnp.sum(jnp.sum(weighted * misfit, axis=1, keepdims=True), axis=0, keepdims=True)
    loss = loss / count / (2.0 * PAIRS * TOK * 16)
    dpred = (LOSS_SCALE / count) * (weighted + mpair * (both - tgt_p[...]))
    dlogit = (dpred * gate).astype(bf16)

    for a in range(4):
        part = dot(dlogit, headp[a], NT) * (1.0 / POOL)
        dyp_s[a] = part.astype(bf16)
    dyp_r[y] = dyp_s[y]
    dyp_in = [copies.start(dyp_s.at[turn(y, o)], dyp_r.at[y], at_y(o)) for o in offs]
    for h in range(HEADS):
        part = dot(dlogit, head[C + h * VD : C + h * VD + VP, :], NT)
        datt_s[h] = jnp.where(lane < VD, part, 0.0).astype(bf16)
    datt_r[zl] = datt_s[zl]
    datt_in = [
        copies.start(datt_s.at[turn(zl, o)], datt_r.at[zl], at_zl(o)) for o in offs
    ]
    dyt[8 : 8 + TOK, :] = dot(dlogit, head[0:C, :], NT) * (1.0 / POOL)

    g_weigh.end()
    for o, n in zip(offs, dyp_in):
        copies.arrived(n, dyp_r.at[turn(y, 4 - o)])
    @pl.loop(0, 4)
    def _(b):
        cols = pl.ds(pl.multiple_of(b * 256, 256), 256)
        gains = jnp.zeros((4 * TOK, 256), f32)
        dyr = dyp_r[...].reshape(4 * TOK, 256)
        for t in range(KW):
            part = pl.ds(t * TOK, TOK)
            w = wf[t, :, :, :, :, cols].reshape(256, 256)
            acc = dot(dyr, w, NN)
            zp_s[:, part, cols] = acc.astype(bf16).reshape(4, TOK, 256)
            gains = gains + acc * weigh[:, part, cols].reshape(4 * TOK, 256).astype(f32)
        gacc[:, cols] = jnp.sum(gains, axis=0, keepdims=True)

    zp_in = [copies.start(zp_s.at[turn(y, o)], zp_r.at[y], at_y(o)) for o in offs]
    zp_r[y] = zp_s[y]

    def all_sum(buf, mine, total, device):
        buf[mine] = total
        return [copies.start(buf.at[mine], buf.at[mine], device(o)) for o in offs]

    def sum_of(buf, mine, ins):
        for o, n in zip(offs, ins):
            copies.arrived(n, buf.at[turn(mine, 4 - o)])
        return (buf[0] + buf[1]) + (buf[2] + buf[3])

    ar_c[c] = jnp.concatenate([gacc[...], jnp.broadcast_to(loss, (1, 128))], axis=1)
    ar_in = copies.start(ar_c.at[c], ar_c.at[c], other)
    for o, n in zip(offs, datt_in):
        copies.arrived(n, datt_r.at[turn(zl, 4 - o)])
    dout = datt_r[...].reshape(4 * TOK, VP)
    att = att_s[...].reshape(4 * TOK, VP)
    delta = jnp.sum(dout.astype(f32) * att.astype(f32), axis=1, keepdims=True)
    vh = kva[:, :, :, 2 * QK :].reshape(16 * TOK, VP)
    ds = (probs[...] * (dot(dout, vh, NT) - delta)).astype(bf16)
    qh = kva[x, :, :, 0:QK].reshape(4 * TOK, QK)
    kvp_s[:, :, :, 0:QK] = dot(ds, qh, TN).astype(bf16).reshape(4, 4, TOK, QK)
    kvp_s[:, :, :, QK:] = dot(probs_b[...], dout, TN).astype(bf16).reshape(4, 4, TOK, VP)
    kvp_in = [copies.start(kvp_s.at[turn(x, o)], kvp_r.at[x], at_x(o)) for o in offs]
    kh = kva[:, :, :, QK : 2 * QK].reshape(16 * TOK, QK)
    dq_s[...] = (dot(ds, kh, NN) * inv_sqrt).astype(bf16).reshape(4, TOK, QK)
    dq_r[zl] = dq_s[zl]
    dq_in = [copies.start(dq_s.at[turn(zl, o)], dq_r.at[zl], at_zl(o)) for o in offs]
    copies.arrived(ar_in, ar_c.at[1 - c])
    ar_in = all_sum(ar_h, zh, ar_c[0] + ar_c[1], at_zh)

    for o, n in zip(offs, kvp_in):
        copies.arrived(n, kvp_r.at[turn(x, 4 - o)])
    total = kvp_s[x].astype(f32)
    for o in offs:
        total = total + kvp_r[turn(x, o)].astype(f32)
    kvg_s[:, :, 0:QK] = (total[:, :, 0:QK] * inv_sqrt).astype(bf16)
    kvg_s[:, :, QK:] = total[:, :, QK:].astype(bf16)
    kvg_r[zl] = kvg_s[zl]
    kvg_in = [
        copies.start(kvg_s.at[turn(zl, o)], kvg_r.at[zl], at_zl(o)) for o in offs
    ]
    ar_in = all_sum(ar_l, zl, sum_of(ar_h, zh, ar_in), at_zl)
    for o, n in zip(offs, zp_in):
        copies.arrived(n, zp_r.at[turn(y, 4 - o)])

    @pl.loop(0, 4)
    def _(b):
        cols = pl.ds(pl.multiple_of(b * 256, 256), 256)
        for t in range(KW):
            part = pl.ds(t * TOK, TOK)
            low = zp_r[0, part, cols].astype(f32) + zp_r[1, part, cols].astype(f32)
            high = zp_r[2, part, cols].astype(f32) + zp_r[3, part, cols].astype(f32)
            zall[t, 8 : 8 + TOK, cols] = low + high

    for t in range(KW):
        rim_s[0, t : t + 1, :] = zall[t, 8:9, :]
        rim_s[1, t : t + 1, :] = zall[t, 7 + TOK : 8 + TOK, :]
    rim_s[0, KW : KW + 1, :] = dyt[8:9, :]
    rim_s[1, KW : KW + 1, :] = dyt[7 + TOK : 8 + TOK, :]
    rim_hi = copies.start(rim_s.at[0], rim_r.at[0], before)
    rim_lo = copies.start(rim_s.at[1], rim_r.at[1], after)
    copies.arrived(rim_hi, rim_r.at[0])
    copies.arrived(rim_lo, rim_r.at[1])
    ar_p[x, y] = sum_of(ar_l, zl, ar_in)
    plane = [(a, b) for a in range(4) for b in range(4) if a or b]
    ar_in = [
        copies.start(ar_p.at[x, y], ar_p.at[x, y], at_xy(a, b)) for a, b in plane
    ]
    for t in range(KW):
        zall[t, 7:8, :] = rim_r[1, t : t + 1, :]
        zall[t, 8 + TOK : 9 + TOK, :] = rim_r[0, t : t + 1, :]
    dyt[7:8, :] = rim_r[1, KW : KW + 1, :]
    dyt[8 + TOK : 9 + TOK, :] = rim_r[0, KW : KW + 1, :]

    @pl.loop(0, 4)
    def _(b):
        cols = pl.ds(pl.multiple_of(b * 256, 256), 256)

        def exact(mat, val):
            top = val.astype(bf16)
            low = (val - top.astype(f32)).astype(bf16)
            return dot(mat, top, NN) + dot(mat, low, NN)

        dhb[:, cols] = exact(three[...], zall[:, :, cols].reshape(KW * 64, 256))
        dyb[:, cols] = exact(one[...], dyt[:, cols])

    @pl.loop(0, ROWS // 16)
    def _(i):
        at = pl.ds(pl.multiple_of(i * 16, 16), 16)
        n = nbuf[at, :]
        dn = dhb[at, :] * dbuf[at, :]
        mid = jnp.mean(dn * n, axis=1, keepdims=True)
        r = rbuf[at, :][:, 0:1]
        dfeats[at, :] = (r * (dn - n * mid) + dyb[at, :]).astype(bf16)

    for o, n in zip(offs, dq_in):
        copies.arrived(n, dq_r.at[turn(zl, 4 - o)])
    for h in range(HEADS):
        dquery[:, h * QK : (h + 1) * QK] = dq_r[h]
    for o, n in zip(offs, kvg_in):
        copies.arrived(n, kvg_r.at[turn(zl, 4 - o)])
    for h in range(HEADS):
        dkey[:, h * QK : (h + 1) * QK] = kvg_r[h, :, 0:QK]
    for h in (0, 2):
        even = kvg_r[h, :, QK:].astype(f32)
        odd = pltpu.roll(kvg_r[h + 1, :, QK:].astype(f32), VD, 1)
        start = h * VD
        dvalue[:, start : start + VP] = jnp.where(lane < VD, even, odd).astype(bf16)
        dvalue[:, start + VP : start + VP + 128] = odd[:, 0:128].astype(bf16)

    for (a, b), n in zip(plane, ar_in):
        copies.arrived(n, ar_p.at[turn(x, 4 - a), turn(y, 4 - b)])
    total = jnp.zeros((1, ROW), f32)
    for a in range(4):
        total = total + ((ar_p[a, 0] + ar_p[a, 1]) + (ar_p[a, 2] + ar_p[a, 3]))
    dgain[...] = total[:, 0:C]
    loss_out[...] = total[:, C:]
    copies.finish()


def store_kernel(*refs):
    sems = refs[12]
    puts = [pltpu.make_async_copy(refs[i], refs[6 + i], sems.at[i]) for i in range(6)]
    for put in puts:
        put.start()
    for put in puts:
        put.wait()


def body(
    features,
    shift_offsets,
    conv_weight,
    norm_gain,
    query_proj,
    key_proj,
    value_proj,
    head_weight,
    targets,
    track_mask,
    track_pairing,
):
    wt = jnp.swapaxes(conv_weight, 1, 2).reshape(KW, 2, 16, C)
    vmem = pl.BlockSpec(memory_space=pltpu.VMEM)
    hbm = pl.BlockSpec(memory_space=pltpu.HBM)
    V = pltpu.VMEM
    scratch = [
        V((1, PAIRS), jnp.int32),
        V((1, C), f32),
        V((TOK, HEADS * VD), bf16),
        V((TOK, TRACKS), f32),
        V((PAIRS, TRACKS), jnp.int32),
        V((1, TRACKS), jnp.int32),
        V((KW, 4, 2, 2, 16, C), bf16),
        V((ROWS + 2 * RIM, C), bf16),
        V((ROWS + 2 * RIM, C), bf16),
        V((ROWS + 2 * RIM, C), bf16),
        V((ROWS + 2 * RIM, C), bf16),
        V((ROWS, C), f32),
        V((ROWS, C), f32),
        V((ROWS, 128), f32),
        V((C + HEADS * VD + VP - VD, TRACKS), bf16),
        V((4, 256, TRACKS), bf16),
        V((4, TOK, 512), bf16),
        V((4, 4, TOK, 512), bf16),
        V((4, TOK, VP), bf16),
        V((4, TOK, VP), bf16),
        V((4 * TOK, 16 * TOK), f32),
        V((4 * TOK, 16 * TOK), bf16),
        V((4, KW * TOK, C), bf16),
        V((4, KW * TOK, C), bf16),
        V((4, TOK, 256), bf16),
        V((4, TOK, 256), bf16),
        V((4, TOK, 256), bf16),
        V((4, TOK, 256), bf16),
        V((4, KW * TOK, C), bf16),
        V((4, KW * TOK, C), bf16),
        V((TOK, TRACKS), f32),
        V((TOK, TRACKS), bf16),
        V((TOK, TRACKS), bf16),
        V((TOK, TRACKS), bf16),
        V((TOK, TRACKS), bf16),
        V((TRACKS, TRACKS), bf16),
        V((TOK, TRACKS), f32),
        V((ROWS, KW * 64), bf16),
        V((ROWS, 64), bf16),
        V((4, TOK, VP), bf16),
        V((4, TOK, VP), bf16),
        V((4, TOK, QK), bf16),
        V((4, TOK, QK), bf16),
        V((4, 4, TOK, 384), bf16),
        V((4, 4, TOK, 384), bf16),
        V((4, TOK, 384), bf16),
        V((4, TOK, 384), bf16),
        V((64, C), f32),
        V((KW, 64, C), f32),
        V((2, 8, C), f32),
        V((2, 8, C), f32),
        V((ROWS, C), f32),
        V((ROWS, C), f32),
        V((1, C), f32),
        V((2, 1, ROW), f32),
        V((4, 4, 1, ROW), f32),
        V((4, 1, ROW), f32),
        V((4, 1, ROW), f32),
        pltpu.SemaphoreType.DMA((COPIES,)),
        pltpu.SemaphoreType.DMA((COPIES,)),
        pltpu.SemaphoreType.DMA((36,)),
    ]
    out = jax.ShapeDtypeStruct
    outs = pl.pallas_call(
        step_kernel,
        name="strand_step",
        out_shape=(
            out((ROWS, C), bf16),
            out((TOK, HEADS * QK), bf16),
            out((TOK, HEADS * QK), bf16),
            out((TOK, HEADS * VD), bf16),
            out((1, C), f32),
            out((1, 128), f32),
        ),
        in_specs=[hbm] * 11,
        out_specs=(vmem,) * 6,
        scratch_shapes=scratch,
        compiler_params=pltpu.CompilerParams(
            collective_id=0, has_side_effects=True, vmem_limit_bytes=48 << 20
        ),
    )(
        *(
            pltpu.with_memory_space_constraint(a, pltpu.HBM)
            for a in (
                features[0],
                shift_offsets.reshape(1, PAIRS),
                wt,
                norm_gain.reshape(1, C),
                query_proj[0],
                key_proj[0],
                value_proj[0],
                head_weight,
                targets[0],
                track_mask,
                track_pairing.reshape(1, TRACKS),
            )
        )
    )
    outs = pl.pallas_call(
        store_kernel,
        name="store",
        out_shape=tuple(out(o.shape, o.dtype) for o in outs),
        in_specs=[vmem] * 6,
        out_specs=(hbm,) * 6,
        scratch_shapes=[pltpu.SemaphoreType.DMA((6,))],
        compiler_params=pltpu.CompilerParams(vmem_limit_bytes=4 << 20),
    )(*outs)
    features_grad, query_grad, key_grad, value_grad, gain_grad, loss = outs
    return (
        features_grad[None],
        query_grad[None],
        key_grad[None],
        value_grad[None],
        gain_grad.reshape(C),
        loss[0, 0],
    )


def solution(mesh):
    placed = (
        P("dp", "seq", None),
        P(),
        P(None, None, "dp"),
        P(),
        P("dp", "seq", None),
        P("dp", "seq", None),
        P("dp", "seq", None),
        P(),
        P("dp", "seq", None),
        P(),
        P(),
    )
    return jax.shard_map(
        body,
        mesh=mesh,
        in_specs=placed,
        out_specs=(
            P("dp", "seq", None),
            P("dp", "seq", None),
            P("dp", "seq", None),
            P("dp", "seq", None),
            P(),
            P(),
        ),
        check_vma=False,
    )
```

time: 98.3 us -> 79.2 us (0.81); the launches traced: 96.5 us -> 78.5 us
  Pallas kernels: 95.9 us -> 77.8 us
    pallas_call x1, Pallas kernels: 95 us -> 77 us  [body(): pl.pallas_call(step_kernel, name='strand_step', out_shape=(out((ROWS, C),...]
where the time goes in v2:
time: 79.2 us; the launch traced here: 78.5 us
  Pallas kernels  77.8 us (98%)
    pallas_call x1, Pallas kernels, body(): pl.pallas_call(step_kernel, name='strand_step', out_shape=(out((ROWS, C),...  77 us

profile of v2, /device:TPU:1, one launch (start us, length us, event | category | flops | bytes accessed | tf_op | source)
XLA Modules:
  0.0 78.5 jit_solution(11168795957175500259)
XLA Ops:
  0.6 77.0 %strand_step.1 = (bf16[256,1024]{1,0:T(8,128)(2,1)S(1)}, bf16[32,512]{1,0:T(8,128)(2,1)S(1)}, bf16[32,512]{1,0:T(8,128)(2,1)S(1)}, bf16[32,768]{1,0:T(8,128)(2,1...) custom-call(bf16[256,1024]{1,0:T(8,128)(2,1)} %bitcast.18, s32[1,16]{1,0:T(1,128)} %bitcast.26, ...), custom_call_target="tpu_custom_call" | custom-call | tf_op jit(solution)/shard_map/strand_step/pallas_call | solution.py:729
  77.6 0.9 %store.1 = (bf16[256,1024]{1,0:T(8,128)(2,1)}, bf16[32,512]{1,0:T(8,128)(2,1)}, bf16[32,512]{1,0:T(8,128)(2,1)}, bf16[32,768]{1,0:T(8,128)(2,1)}, f32[1,1024]{1,0:T(1,128)}, /*index=5*/f32[1,128]{1,0:T(1,128)}) custom-call(bf16[256,1024]{1,0:T(8,128)(2,1)S(1)} %get-tuple-element.18.refs_0_, bf16[32,512]{1,0:T(8,128)(2,1)S(1)} %get-tuple-element.19.refs_1_, ...), custom_call_target="tpu_custom_call" | custom-call | tf_op jit(solution)/shard_map/store/pallas_call | solution.py:764

commit v3 on v2

--- a/solution.py
+++ b/solution.py
@@ -26,7 +26,7 @@
 LOSS_SCALE = 1024.0
 ROOT = math.sqrt(2.0 / math.pi)
 CUBIC = 0.044715
-COPIES = 136
+COPIES = 121
 f32 = jnp.float32
 bf16 = jnp.bfloat16
 
@@ -73,6 +73,7 @@
         ).wait_recv()
 
     def finish(self):
+        assert self.used <= COPIES
         for copy in self.sent:
             copy.wait_send()
 
@@ -189,8 +190,7 @@
     gacc,
     ar_c,
     ar_p,
-    ar_l,
-    ar_h,
+    ar_z,
     send_sem,
     recv_sem,
     own_sem,
@@ -220,7 +220,8 @@
     before = {"dp": dp, "seq": lax.rem(s + 15, 16)}
 
     barrier = pltpu.get_barrier_semaphore()
-    peers = [f(o) for f in (at_y, at_zh, at_x, at_zl) for o in (1, 2, 3)]
+    peers = [f(o) for f in (at_y, at_x, at_zl) for o in (1, 2, 3)]
+    peers += [at_zh(1), at_zh(3)]
     peers += [other, after, before]
     offs = (1, 2, 3)
 
@@ -228,6 +229,13 @@
         return {"dp": zh * 8 + turn(y, b) * 2 + c, "seq": turn(x, a) * 4 + zl}
 
     peers += [at_xy(a, b) for a in offs for b in offs]
+
+    def around(o):
+        return lax.rem(zh * 4 + zl + o, 16)
+
+    def at_z(o):
+        z = around(o)
+        return {"dp": lax.div(z, 4) * 8 + y * 2 + c, "seq": x * 4 + lax.rem(z, 4)}
     for peer in peers:
         pl.semaphore_signal(
             barrier, inc=1, device_id=peer, device_id_type=pl.DeviceIdType.MESH
@@ -242,7 +250,7 @@
         pulls[-1].start()
         return pulls[-1]
 
-    wt_pull = pull(wt_in, wf.at[:, zh, c])
+    wt_pull = pull(wt_in, wf.at[:, 0, c])
     qkv_pulls = [pull(value_in, value)]
     for h in range(HEADS):
         cols = pl.ds(h * QK, QK)
@@ -259,7 +267,8 @@
     head_copies = [pull(head_in, head.at[pl.ds(0, rows)])]
     for a in range(4):
         for b in range(4):
-            block = head_in.at[pl.ds(256 * b + 64 * a, 64)]
+            start = pl.multiple_of(256 * turn(zh, b) + 64 * a, 64)
+            block = head_in.at[pl.ds(start, 64)]
             head_copies.append(pull(block, headp.at[a, pl.ds(64 * b, 64)]))
     fext[0:8, :] = jnp.zeros((8, C), bf16)
     fext[2 * RIM + ROWS - 8 :, :] = jnp.zeros((8, C), bf16)
@@ -270,13 +279,13 @@
             return pl.ds(pl.multiple_of(turn(x, o) * 256, 128), 256)
         return pl.ds(pl.multiple_of(turn(x, o) * 256 + 128 * half, 128), 128)
 
-    def unit_z(o, half):
+    def slot(t, r, half):
         if half is None:
-            return wf.at[:, turn(zh, o), c, :, :, columns(0, None)]
-        return wf.at[:, turn(zh, o), c, half, :, columns(0, None)]
-
-    def unit_yx(r):
-        return lambda o, half: wf.at[:, turn(zh, r), c, :, :, columns(o, half)]
+            return wf.at[t, r, c, :, :, columns(0, None)]
+        return wf.at[t, r, c, half, :, columns(0, None)]
+
+    def unit_yx(t, r):
+        return lambda o, half: wf.at[t, r, c, :, :, columns(o, half)]
 
     def unit_of(buf):
         def unit(o, half):
@@ -293,8 +302,7 @@
             return kva.at[turn(x, o), :, :, kv_cols]
         return kva.at[turn(x, o), pl.ds(2 * half, 2), :, kv_cols]
 
-    g_z = Gather(copies, at_zh, unit_z)
-    g_yx = [Direct(copies, at_x, unit_yx(r)) for r in range(4)]
+    g_yx = [[Direct(copies, at_x, unit_yx(t, r)) for r in range(4)] for t in range(KW)]
     g_taps = Gather(copies, at_y, unit_of(taps))
     g_weigh = Gather(copies, at_y, unit_of(weigh))
     g_kv = Direct(copies, at_x, unit_kv)
@@ -305,12 +313,18 @@
     edge = pl.ds(RIM + ROWS, 8)
     lo = copies.start(fext.at[pl.ds(ROWS + 8, 8)], fext.at[pl.ds(8, 8)], after)
     hi = copies.start(fext.at[pl.ds(RIM, 8)], fext.at[edge], before)
-    g_z.begin()
+    z_in = []
+    for t in range(KW):
+        right = copies.start(slot(t, 0, None), slot(t, 3, None), at_zh(1))
+        left = copies.start(slot(t, 0, None), slot(t, 1, None), at_zh(3))
+        z_in.append((right, left))
     pair_in = []
 
-    def share(r):
-        part = wf.at[:, turn(zh, r), c]
-        pair_in.append((copies.start(part, part, other), wf.at[:, turn(zh, r), 1 - c]))
+    def share(r, t=None):
+        taps_of = pl.ds(0, KW) if t is None else t
+        part = wf.at[taps_of, r, c]
+        n = copies.start(part, part, other)
+        pair_in.append((r, n, wf.at[taps_of, r, 1 - c]))
 
     share(0)
 
@@ -329,32 +343,33 @@
     qkv_in = [
         copies.start(qkv.at[turn(zl, o)], kva.at[x, zl], at_zl(o)) for o in offs
     ]
-    def pointwise(row):
-        at = pl.ds(row, 16)
-        f = fext[at, :].astype(f32)
+    def normed(row):
+        f = fext[pl.ds(row, 16), :].astype(f32)
         r = lax.rsqrt(jnp.mean(f * f, axis=1, keepdims=True) + NORM_EPS)
         n = f * r
         g = n * gain[...]
         sq = g * g
         t = jnp.tanh(ROOT * (g + CUBIC * (sq * g)))
-        hext[at, :] = (0.5 * g * (1.0 + t)).astype(bf16)
+        return n, g, sq, t, r
+
+    def hidden(row):
+        n, g, sq, t, r = normed(row)
+        hext[pl.ds(row, 16), :] = (0.5 * g * (1.0 + t)).astype(bf16)
+
+    def slopes(row):
+        n, g, sq, t, r = normed(row)
         slope = 0.5 * (1.0 + t) + (0.5 * ROOT) * g * (1.0 - t * t) * (
             1.0 + (3.0 * CUBIC) * sq
         )
         dn = slope * n
         top = dn.astype(bf16)
-        dnh[at, :] = top
-        dnl[at, :] = (dn - top.astype(f32)).astype(bf16)
+        dnh[pl.ds(row, 16), :] = top
+        dnl[pl.ds(row, 16), :] = (dn - top.astype(f32)).astype(bf16)
         return n, slope, r
 
-    @pl.loop(0, ROWS // 16)
+    @pl.loop(1, 1 + ROWS // 16)
     def _(i):
-        row = pl.multiple_of(i * 16, 16)
-        n, slope, r = pointwise(pl.multiple_of(row + RIM, 16))
-        nbuf[pl.ds(row, 16), :] = n
-        dbuf[pl.ds(row, 16), :] = slope * gain[...]
-        rbuf[pl.ds(row, 16), :] = jnp.broadcast_to(r, (16, 128))
-
+        hidden(pl.multiple_of(i * 16, 16))
 
     for pulled in rest_pulls:
         pulled.wait()
@@ -382,20 +397,38 @@
     still = mean_matrix(TOK, lambda row: 0 * row)
     copies.arrived(lo, fext.at[pl.ds(8, 8)])
     copies.arrived(hi, fext.at[edge])
-    pointwise(0)
-    pointwise(RIM + ROWS)
+    hidden(0)
+    hidden(RIM + ROWS)
     taps[y] = dot(mix, hext[...], NN).astype(bf16)
     g_taps.begin()
-    weigh[y] = ((dot(mix, dnh[...], NN) + dot(mix, dnl[...], NN)) * POOL).astype(bf16)
     pooled_u = dot(still, fext[...], NN).astype(bf16)
+
+    def later(first, last):
+        @pl.loop(first, last)
+        def _(i):
+            row = pl.multiple_of(i * 16, 16)
+            n, slope, r = slopes(pl.multiple_of(row + RIM, 16))
+            nbuf[pl.ds(row, 16), :] = n
+            dbuf[pl.ds(row, 16), :] = slope * gain[...]
+            rbuf[pl.ds(row, 16), :] = jnp.broadcast_to(r, (16, 128))
+
+    z_far = []
+    for t in range(KW):
+        right, left = z_in[t]
+        copies.arrived(right, slot(t, 3, None))
+        to_right = copies.start(slot(t, 3, 0), slot(t, 2, 0), at_zh(1))
+        g_yx[t][3].begin()
+        copies.arrived(left, slot(t, 1, None))
+        to_left = copies.start(slot(t, 1, 1), slot(t, 2, 1), at_zh(3))
+        g_yx[t][1].begin()
+        z_far.append((to_right, to_left))
+    for o, n in zip(offs, qkv_in):
+        copies.arrived(n, kva.at[x, turn(zl, 4 - o)])
+    g_kv.begin()
+    g_taps.relay()
     for pulled in head_copies:
         pulled.wait()
     pre[...] = dot(pooled_u, head[0:C, :], NN)
-
-    g_z.relay_from_left()
-    g_yx[3].begin()
-    g_z.relay_from_right()
-    g_yx[1].begin()
     def spread(width, tap_of):
         row, col = iota((ROWS, width), 0), iota((ROWS, width), 1)
         reach = row + off - tap_of(col)
@@ -411,21 +444,34 @@
     zall[...] = jnp.zeros((KW, 64, C), f32)
     rim_s[...] = jnp.zeros((2, 8, C), f32)
 
-    g_taps.relay()
-    g_z.end()
-    g_yx[2].begin()
-    for o, n in zip(offs, qkv_in):
-        copies.arrived(n, kva.at[x, turn(zl, 4 - o)])
-    g_kv.begin()
+    later(0, 8)
+    for t in range(KW):
+        to_right, to_left = z_far[t]
+        copies.arrived(to_right, slot(t, 2, 0))
+        copies.arrived(to_left, slot(t, 2, 1))
+        g_yx[t][2].begin()
     tgt_s[...] = targets[...].astype(bf16)
     tgt_in = copies.start(tgt_s, tgt_r, at_zh(2))
-    g_yx[3].end()
-    share(3)
-    g_yx[1].end()
-    share(1)
+    for r in (3, 1):
+        for t in range(KW):
+            g_yx[t][r].end()
+        share(r)
+    slopes(0)
+    slopes(RIM + ROWS)
+    later(8, 16)
     g_taps.end()
-    g_yx[2].end()
-    share(2)
+
+    def convolve(r):
+        for q, n, part in pair_in:
+            if q == r:
+                copies.arrived(n, part)
+        acc = jnp.zeros((4 * TOK, 64), f32)
+        for t in range(KW):
+            rows_t = taps[:, t * TOK : (t + 1) * TOK, :].reshape(4 * TOK, C)
+            acc = acc + dot(rows_t, wf[t, r].reshape(64, C), NT)
+        cv_s[:, :, r * 64 : (r + 1) * 64] = acc.astype(bf16).reshape(4, TOK, 64)
+
+    convolve(0)
     g_kv.end()
     inv_sqrt = 1.0 / math.sqrt(QK)
     qh = kva[x, :, :, 0:QK].reshape(4 * TOK, QK)
@@ -441,16 +487,16 @@
     att_in = [
         copies.start(att_s.at[turn(zl, o)], att_r.at[zl], at_zl(o)) for o in offs
     ]
-    for n, part in pair_in:
-        copies.arrived(n, part)
-
-    acc = jnp.zeros((4 * TOK, 256), f32)
     for t in range(KW):
-        rows_t = taps[:, t * TOK : (t + 1) * TOK, :].reshape(4 * TOK, C)
-        acc = acc + dot(rows_t, wf[t].reshape(256, C), NT)
-    cv_s[...] = acc.astype(bf16).reshape(4, TOK, 256)
+        g_yx[t][2].end()
+        share(2, t)
+    convolve(3)
+    convolve(1)
+    convolve(2)
     cv_r[y] = cv_s[y]
     cv_in = [copies.start(cv_s.at[turn(y, o)], cv_r.at[y], at_y(o)) for o in offs]
+    both = dot(mix, dnh[...], NN) + dot(mix, dnl[...], NN)
+    weigh[y] = (both * POOL).astype(bf16)
     g_weigh.begin()
     pick[...] = jnp.where(
         iota((TRACKS, TRACKS), 0) == pairing[...], 1.0, 0.0
@@ -479,8 +525,6 @@
     both = 0.5 * (pred + dot(pred_r[...], pick[...], NN))
     misfit = both - targets[...]
     weighted = mrow * misfit
-    loss = jnp.sum(jnp.sum(weighted * misfit, axis=1, keepdims=True), axis=0, keepdims=True)
-    loss = loss / count / (2.0 * PAIRS * TOK * 16)
     dpred = (LOSS_SCALE / count) * (weighted + mpair * (both - tgt_p[...]))
     dlogit = (dpred * gate).astype(bf16)
 
@@ -498,6 +542,8 @@
     ]
     dyt[8 : 8 + TOK, :] = dot(dlogit, head[0:C, :], NT) * (1.0 / POOL)
 
+    loss = jnp.sum(jnp.sum(weighted * misfit, axis=1, keepdims=True), axis=0, keepdims=True)
+    loss = loss / count / (2.0 * PAIRS * TOK * 16)
     g_weigh.end()
     for o, n in zip(offs, dyp_in):
         copies.arrived(n, dyp_r.at[turn(y, 4 - o)])
@@ -516,15 +562,6 @@
 
     zp_in = [copies.start(zp_s.at[turn(y, o)], zp_r.at[y], at_y(o)) for o in offs]
     zp_r[y] = zp_s[y]
-
-    def all_sum(buf, mine, total, device):
-        buf[mine] = total
-        return [copies.start(buf.at[mine], buf.at[mine], device(o)) for o in offs]
-
-    def sum_of(buf, mine, ins):
-        for o, n in zip(offs, ins):
-            copies.arrived(n, buf.at[turn(mine, 4 - o)])
-        return (buf[0] + buf[1]) + (buf[2] + buf[3])
 
     ar_c[c] = jnp.concatenate([gacc[...], jnp.broadcast_to(loss, (1, 128))], axis=1)
     ar_in = copies.start(ar_c.at[c], ar_c.at[c], other)
@@ -544,7 +581,9 @@
     dq_r[zl] = dq_s[zl]
     dq_in = [copies.start(dq_s.at[turn(zl, o)], dq_r.at[zl], at_zl(o)) for o in offs]
     copies.arrived(ar_in, ar_c.at[1 - c])
-    ar_in = all_sum(ar_h, zh, ar_c[0] + ar_c[1], at_zh)
+    ar_z[around(0)] = ar_c[0] + ar_c[1]
+    ring = (8, 7, 9, 6, 10, 5, 11, 4, 12, 3, 13, 2, 14, 1, 15)
+    ar_in = [copies.start(ar_z.at[around(0)], ar_z.at[around(0)], at_z(o)) for o in ring]
 
     for o, n in zip(offs, kvp_in):
         copies.arrived(n, kvp_r.at[turn(x, 4 - o)])
@@ -557,7 +596,6 @@
     kvg_in = [
         copies.start(kvg_s.at[turn(zl, o)], kvg_r.at[zl], at_zl(o)) for o in offs
     ]
-    ar_in = all_sum(ar_l, zl, sum_of(ar_h, zh, ar_in), at_zl)
     for o, n in zip(offs, zp_in):
         copies.arrived(n, zp_r.at[turn(y, 4 - o)])
 
@@ -577,13 +615,18 @@
     rim_s[1, KW : KW + 1, :] = dyt[7 + TOK : 8 + TOK, :]
     rim_hi = copies.start(rim_s.at[0], rim_r.at[0], before)
     rim_lo = copies.start(rim_s.at[1], rim_r.at[1], after)
-    copies.arrived(rim_hi, rim_r.at[0])
-    copies.arrived(rim_lo, rim_r.at[1])
-    ar_p[x, y] = sum_of(ar_l, zl, ar_in)
+    for o, n in zip(ring, ar_in):
+        copies.arrived(n, ar_z.at[around(16 - o)])
+    total = jnp.zeros((1, ROW), f32)
+    for a in range(0, 16, 4):
+        total = total + ((ar_z[a] + ar_z[a + 1]) + (ar_z[a + 2] + ar_z[a + 3]))
+    ar_p[x, y] = total
     plane = [(a, b) for a in range(4) for b in range(4) if a or b]
     ar_in = [
         copies.start(ar_p.at[x, y], ar_p.at[x, y], at_xy(a, b)) for a, b in plane
     ]
+    copies.arrived(rim_hi, rim_r.at[0])
+    copies.arrived(rim_lo, rim_r.at[1])
     for t in range(KW):
         zall[t, 7:8, :] = rim_r[1, t : t + 1, :]
         zall[t, 8 + TOK : 9 + TOK, :] = rim_r[0, t : t + 1, :]
@@ -719,8 +762,7 @@
         V((1, C), f32),
         V((2, 1, ROW), f32),
         V((4, 4, 1, ROW), f32),
-        V((4, 1, ROW), f32),
-        V((4, 1, ROW), f32),
+        V((16, 1, ROW), f32),
         pltpu.SemaphoreType.DMA((COPIES,)),
         pltpu.SemaphoreType.DMA((COPIES,)),
         pltpu.SemaphoreType.DMA((36,)),

time: 79.2 us -> 72.5 us (0.915)
  Pallas kernels: 77.8 us -> 70.5 us
    pallas_call x1, Pallas kernels: 77 us -> 69.7 us  [body(): pl.pallas_call(step_kernel, name='strand_step', out_shape=(out((ROWS, C),...]
where the time goes in v3:
time: 72.5 us; the launch traced here: 71.2 us
  Pallas kernels  70.5 us (97%)
    pallas_call x1, Pallas kernels, body(): pl.pallas_call(step_kernel, name='strand_step', out_shape=(out((ROWS, C),...  69.7 us

profile of v3, /device:TPU:1, one launch (start us, length us, event | category | flops | bytes accessed | tf_op | source)
XLA Modules:
  0.0 71.2 jit_solution(6745318583010295068)
XLA Ops:
  0.6 69.7 %strand_step.1 = (bf16[256,1024]{1,0:T(8,128)(2,1)S(1)}, bf16[32,512]{1,0:T(8,128)(2,1)S(1)}, bf16[32,512]{1,0:T(8,128)(2,1)S(1)}, bf16[32,768]{1,0:T(8,128)(2,1...) custom-call(bf16[256,1024]{1,0:T(8,128)(2,1)} %bitcast.18, s32[1,16]{1,0:T(1,128)} %bitcast.26, ...), custom_call_target="tpu_custom_call" | custom-call | tf_op jit(solution)/shard_map/strand_step/pallas_call | solution.py:771
  70.3 0.9 %store.1 = (bf16[256,1024]{1,0:T(8,128)(2,1)}, bf16[32,512]{1,0:T(8,128)(2,1)}, bf16[32,512]{1,0:T(8,128)(2,1)}, bf16[32,768]{1,0:T(8,128)(2,1)}, f32[1,1024]{1,0:T(1,128)}, /*index=5*/f32[1,128]{1,0:T(1,128)}) custom-call(bf16[256,1024]{1,0:T(8,128)(2,1)S(1)} %get-tuple-element.18.refs_0_, bf16[32,512]{1,0:T(8,128)(2,1)S(1)} %get-tuple-element.19.refs_1_, ...), custom_call_target="tpu_custom_call" | custom-call | tf_op jit(solution)/shard_map/store/pallas_call | solution.py:806

commit v4 on v3

--- a/solution.py
+++ b/solution.py
@@ -26,7 +26,7 @@
 LOSS_SCALE = 1024.0
 ROOT = math.sqrt(2.0 / math.pi)
 CUBIC = 0.044715
-COPIES = 121
+COPIES = 126
 f32 = jnp.float32
 bf16 = jnp.bfloat16
 
@@ -185,6 +185,12 @@
     zall,
     rim_s,
     rim_r,
+    edge_s,
+    edge_r,
+    edges,
+    zr_f,
+    zr_s,
+    zr_r,
     dhb,
     dyb,
     gacc,
@@ -220,15 +226,14 @@
     before = {"dp": dp, "seq": lax.rem(s + 15, 16)}
 
     barrier = pltpu.get_barrier_semaphore()
-    peers = [f(o) for f in (at_y, at_x, at_zl) for o in (1, 2, 3)]
-    peers += [at_zh(1), at_zh(3)]
+    peers = [f(o) for f in (at_x, at_zl) for o in (1, 2, 3)]
+    peers += [f(o) for f in (at_y, at_zh) for o in (1, 3)]
     peers += [other, after, before]
     offs = (1, 2, 3)
 
     def at_xy(a, b):
         return {"dp": zh * 8 + turn(y, b) * 2 + c, "seq": turn(x, a) * 4 + zl}
 
-    peers += [at_xy(a, b) for a in offs for b in offs]
 
     def around(o):
         return lax.rem(zh * 4 + zl + o, 16)
@@ -442,7 +447,8 @@
     one[...] = spread(64, lambda col: 0 * col)
     dyt[...] = jnp.zeros((64, C), f32)
     zall[...] = jnp.zeros((KW, 64, C), f32)
-    rim_s[...] = jnp.zeros((2, 8, C), f32)
+    edges[...] = jnp.zeros((16, 256), f32)
+    zr_f[...] = jnp.zeros((4, 8, C), f32)
 
     later(0, 8)
     for t in range(KW):
@@ -456,9 +462,6 @@
         for t in range(KW):
             g_yx[t][r].end()
         share(r)
-    slopes(0)
-    slopes(RIM + ROWS)
-    later(8, 16)
     g_taps.end()
 
     def convolve(r):
@@ -495,6 +498,9 @@
     convolve(2)
     cv_r[y] = cv_s[y]
     cv_in = [copies.start(cv_s.at[turn(y, o)], cv_r.at[y], at_y(o)) for o in offs]
+    slopes(0)
+    slopes(RIM + ROWS)
+    later(8, 16)
     both = dot(mix, dnh[...], NN) + dot(mix, dnl[...], NN)
     weigh[y] = (both * POOL).astype(bf16)
     g_weigh.begin()
@@ -541,12 +547,22 @@
         copies.start(datt_s.at[turn(zl, o)], datt_r.at[zl], at_zl(o)) for o in offs
     ]
     dyt[8 : 8 + TOK, :] = dot(dlogit, head[0:C, :], NT) * (1.0 / POOL)
+    rim_s[0] = dyt[8:9, :]
+    rim_s[1] = dyt[7 + TOK : 8 + TOK, :]
+    rim_hi = copies.start(rim_s.at[0], rim_r.at[0], before)
+    rim_lo = copies.start(rim_s.at[1], rim_r.at[1], after)
 
     loss = jnp.sum(jnp.sum(weighted * misfit, axis=1, keepdims=True), axis=0, keepdims=True)
     loss = loss / count / (2.0 * PAIRS * TOK * 16)
     g_weigh.end()
     for o, n in zip(offs, dyp_in):
         copies.arrived(n, dyp_r.at[turn(y, 4 - o)])
+    for a in range(4):
+        cols = slice(a * 256, (a + 1) * 256)
+        edge_s[0, :, cols] = dyp_r[a, 0:1, :].astype(f32)
+        edge_s[1, :, cols] = dyp_r[a, TOK - 1 : TOK, :].astype(f32)
+    edge_hi = copies.start(edge_s.at[0], edge_r.at[0], before)
+    edge_lo = copies.start(edge_s.at[1], edge_r.at[1], after)
     @pl.loop(0, 4)
     def _(b):
         cols = pl.ds(pl.multiple_of(b * 256, 256), 256)
@@ -585,6 +601,21 @@
     ring = (8, 7, 9, 6, 10, 5, 11, 4, 12, 3, 13, 2, 14, 1, 15)
     ar_in = [copies.start(ar_z.at[around(0)], ar_z.at[around(0)], at_z(o)) for o in ring]
 
+    copies.arrived(edge_hi, edge_r.at[0])
+    copies.arrived(edge_lo, edge_r.at[1])
+    for a in range(4):
+        cols = slice(a * 256, (a + 1) * 256)
+        edges[a : a + 1, :] = edge_r[0][:, cols]
+        edges[8 + a : 9 + a, :] = edge_r[1][:, cols]
+    both = edges[...].astype(bf16)
+    for t in range(KW):
+        res = dot(both, wf[t].reshape(256, C), NN)
+        for a in range(4):
+            zr_f[a, t : t + 1, :] = res[a : a + 1, :]
+            zr_f[a, KW + t : KW + t + 1, :] = res[8 + a : 9 + a, :]
+    zr_s[...] = zr_f[...].astype(bf16)
+    zr_r[y] = zr_s[y]
+    zr_in = [copies.start(zr_s.at[turn(y, o)], zr_r.at[y], at_y(o)) for o in offs]
     for o, n in zip(offs, kvp_in):
         copies.arrived(n, kvp_r.at[turn(x, 4 - o)])
     total = kvp_s[x].astype(f32)
@@ -596,25 +627,6 @@
     kvg_in = [
         copies.start(kvg_s.at[turn(zl, o)], kvg_r.at[zl], at_zl(o)) for o in offs
     ]
-    for o, n in zip(offs, zp_in):
-        copies.arrived(n, zp_r.at[turn(y, 4 - o)])
-
-    @pl.loop(0, 4)
-    def _(b):
-        cols = pl.ds(pl.multiple_of(b * 256, 256), 256)
-        for t in range(KW):
-            part = pl.ds(t * TOK, TOK)
-            low = zp_r[0, part, cols].astype(f32) + zp_r[1, part, cols].astype(f32)
-            high = zp_r[2, part, cols].astype(f32) + zp_r[3, part, cols].astype(f32)
-            zall[t, 8 : 8 + TOK, cols] = low + high
-
-    for t in range(KW):
-        rim_s[0, t : t + 1, :] = zall[t, 8:9, :]
-        rim_s[1, t : t + 1, :] = zall[t, 7 + TOK : 8 + TOK, :]
-    rim_s[0, KW : KW + 1, :] = dyt[8:9, :]
-    rim_s[1, KW : KW + 1, :] = dyt[7 + TOK : 8 + TOK, :]
-    rim_hi = copies.start(rim_s.at[0], rim_r.at[0], before)
-    rim_lo = copies.start(rim_s.at[1], rim_r.at[1], after)
     for o, n in zip(ring, ar_in):
         copies.arrived(n, ar_z.at[around(16 - o)])
     total = jnp.zeros((1, ROW), f32)
@@ -625,13 +637,29 @@
     ar_in = [
         copies.start(ar_p.at[x, y], ar_p.at[x, y], at_xy(a, b)) for a, b in plane
     ]
+    for o, n in zip(offs, zp_in):
+        copies.arrived(n, zp_r.at[turn(y, 4 - o)])
+
+    @pl.loop(0, 4)
+    def _(b):
+        cols = pl.ds(pl.multiple_of(b * 256, 256), 256)
+        for t in range(KW):
+            part = pl.ds(t * TOK, TOK)
+            low = zp_r[0, part, cols].astype(f32) + zp_r[1, part, cols].astype(f32)
+            high = zp_r[2, part, cols].astype(f32) + zp_r[3, part, cols].astype(f32)
+            zall[t, 8 : 8 + TOK, cols] = low + high
+
     copies.arrived(rim_hi, rim_r.at[0])
     copies.arrived(rim_lo, rim_r.at[1])
+    for o, n in zip(offs, zr_in):
+        copies.arrived(n, zr_r.at[turn(y, 4 - o)])
+    low = zr_r[0].astype(f32) + zr_r[1].astype(f32)
+    beside = low + (zr_r[2].astype(f32) + zr_r[3].astype(f32))
     for t in range(KW):
-        zall[t, 7:8, :] = rim_r[1, t : t + 1, :]
-        zall[t, 8 + TOK : 9 + TOK, :] = rim_r[0, t : t + 1, :]
-    dyt[7:8, :] = rim_r[1, KW : KW + 1, :]
-    dyt[8 + TOK : 9 + TOK, :] = rim_r[0, KW : KW + 1, :]
+        zall[t, 8 + TOK : 9 + TOK, :] = beside[t : t + 1, :]
+        zall[t, 7:8, :] = beside[KW + t : KW + t + 1, :]
+    dyt[7:8, :] = rim_r[1]
+    dyt[8 + TOK : 9 + TOK, :] = rim_r[0]
 
     @pl.loop(0, 4)
     def _(b):
@@ -755,8 +783,14 @@
         V((4, TOK, 384), bf16),
         V((64, C), f32),
         V((KW, 64, C), f32),
-        V((2, 8, C), f32),
-        V((2, 8, C), f32),
+        V((2, 1, C), f32),
+        V((2, 1, C), f32),
+        V((2, 1, C), f32),
+        V((2, 1, C), f32),
+        V((16, 256), f32),
+        V((4, 8, C), f32),
+        V((4, 8, C), bf16),
+        V((4, 8, C), bf16),
         V((ROWS, C), f32),
         V((ROWS, C), f32),
         V((1, C), f32),

time: 72.5 us -> 71.1 us (0.981)
    pallas_call x1, Pallas kernels: 69.7 us -> 68.9 us  [body(): pl.pallas_call(step_kernel, name='strand_step', out_shape=(out((ROWS, C),...]
where the time goes in v4:
time: 71.1 us; the launch traced here: 70.4 us
  Pallas kernels  69.8 us (98%)
    pallas_call x1, Pallas kernels, body(): pl.pallas_call(step_kernel, name='strand_step', out_shape=(out((ROWS, C),...  68.9 us

profile of v4, /device:TPU:1, one launch (start us, length us, event | category | flops | bytes accessed | tf_op | source)
XLA Modules:
  0.0 70.4 jit_solution(10405832142559931961)
XLA Ops:
  0.6 68.9 %strand_step.1 = (bf16[256,1024]{1,0:T(8,128)(2,1)S(1)}, bf16[32,512]{1,0:T(8,128)(2,1)S(1)}, bf16[32,512]{1,0:T(8,128)(2,1)S(1)}, bf16[32,768]{1,0:T(8,128)(2,1...) custom-call(bf16[256,1024]{1,0:T(8,128)(2,1)} %bitcast.18, s32[1,16]{1,0:T(1,128)} %bitcast.26, ...), custom_call_target="tpu_custom_call" | custom-call | tf_op jit(solution)/shard_map/strand_step/pallas_call | solution.py:805
  69.5 0.9 %store.1 = (bf16[256,1024]{1,0:T(8,128)(2,1)}, bf16[32,512]{1,0:T(8,128)(2,1)}, bf16[32,512]{1,0:T(8,128)(2,1)}, bf16[32,768]{1,0:T(8,128)(2,1)}, f32[1,1024]{1,0:T(1,128)}, /*index=5*/f32[1,128]{1,0:T(1,128)}) custom-call(bf16[256,1024]{1,0:T(8,128)(2,1)S(1)} %get-tuple-element.18.refs_0_, bf16[32,512]{1,0:T(8,128)(2,1)S(1)} %get-tuple-element.19.refs_1_, ...), custom_call_target="tpu_custom_call" | custom-call | tf_op jit(solution)/shard_map/store/pallas_call | solution.py:840

commit v5 on v4

--- a/solution.py
+++ b/solution.py
@@ -26,7 +26,7 @@
 LOSS_SCALE = 1024.0
 ROOT = math.sqrt(2.0 / math.pi)
 CUBIC = 0.044715
-COPIES = 126
+COPIES = 142
 f32 = jnp.float32
 bf16 = jnp.bfloat16
 
@@ -194,7 +194,6 @@
     dhb,
     dyb,
     gacc,
-    ar_c,
     ar_p,
     ar_z,
     send_sem,
@@ -231,8 +230,9 @@
     peers += [other, after, before]
     offs = (1, 2, 3)
 
-    def at_xy(a, b):
-        return {"dp": zh * 8 + turn(y, b) * 2 + c, "seq": turn(x, a) * 4 + zl}
+    def at_xy(a, b, d):
+        core = 1 - c if d else c
+        return {"dp": zh * 8 + turn(y, b) * 2 + core, "seq": turn(x, a) * 4 + zl}
 
 
     def around(o):
@@ -456,8 +456,6 @@
         copies.arrived(to_right, slot(t, 2, 0))
         copies.arrived(to_left, slot(t, 2, 1))
         g_yx[t][2].begin()
-    tgt_s[...] = targets[...].astype(bf16)
-    tgt_in = copies.start(tgt_s, tgt_r, at_zh(2))
     for r in (3, 1):
         for t in range(KW):
             g_yx[t][r].end()
@@ -475,6 +473,9 @@
         cv_s[:, :, r * 64 : (r + 1) * 64] = acc.astype(bf16).reshape(4, TOK, 64)
 
     convolve(0)
+    for t in range(KW):
+        g_yx[t][2].end()
+        share(2, t)
     g_kv.end()
     inv_sqrt = 1.0 / math.sqrt(QK)
     qh = kva[x, :, :, 0:QK].reshape(4 * TOK, QK)
@@ -490,14 +491,13 @@
     att_in = [
         copies.start(att_s.at[turn(zl, o)], att_r.at[zl], at_zl(o)) for o in offs
     ]
-    for t in range(KW):
-        g_yx[t][2].end()
-        share(2, t)
     convolve(3)
     convolve(1)
     convolve(2)
     cv_r[y] = cv_s[y]
     cv_in = [copies.start(cv_s.at[turn(y, o)], cv_r.at[y], at_y(o)) for o in offs]
+    tgt_s[...] = targets[...].astype(bf16)
+    tgt_in = copies.start(tgt_s, tgt_r, at_zh(2))
     slopes(0)
     slopes(RIM + ROWS)
     later(8, 16)
@@ -579,8 +579,11 @@
     zp_in = [copies.start(zp_s.at[turn(y, o)], zp_r.at[y], at_y(o)) for o in offs]
     zp_r[y] = zp_s[y]
 
-    ar_c[c] = jnp.concatenate([gacc[...], jnp.broadcast_to(loss, (1, 128))], axis=1)
-    ar_in = copies.start(ar_c.at[c], ar_c.at[c], other)
+    ar_z[around(0)] = jnp.concatenate(
+        [gacc[...], jnp.broadcast_to(loss, (1, 128))], axis=1
+    )
+    ring = (8, 7, 9, 6, 10, 5, 11, 4, 12, 3, 13, 2, 14, 1, 15)
+    ar_in = [copies.start(ar_z.at[around(0)], ar_z.at[around(0)], at_z(o)) for o in ring]
     for o, n in zip(offs, datt_in):
         copies.arrived(n, datt_r.at[turn(zl, 4 - o)])
     dout = datt_r[...].reshape(4 * TOK, VP)
@@ -596,11 +599,6 @@
     dq_s[...] = (dot(ds, kh, NN) * inv_sqrt).astype(bf16).reshape(4, TOK, QK)
     dq_r[zl] = dq_s[zl]
     dq_in = [copies.start(dq_s.at[turn(zl, o)], dq_r.at[zl], at_zl(o)) for o in offs]
-    copies.arrived(ar_in, ar_c.at[1 - c])
-    ar_z[around(0)] = ar_c[0] + ar_c[1]
-    ring = (8, 7, 9, 6, 10, 5, 11, 4, 12, 3, 13, 2, 14, 1, 15)
-    ar_in = [copies.start(ar_z.at[around(0)], ar_z.at[around(0)], at_z(o)) for o in ring]
-
     copies.arrived(edge_hi, edge_r.at[0])
     copies.arrived(edge_lo, edge_r.at[1])
     for a in range(4):
@@ -632,11 +630,10 @@
     total = jnp.zeros((1, ROW), f32)
     for a in range(0, 16, 4):
         total = total + ((ar_z[a] + ar_z[a + 1]) + (ar_z[a + 2] + ar_z[a + 3]))
-    ar_p[x, y] = total
-    plane = [(a, b) for a in range(4) for b in range(4) if a or b]
-    ar_in = [
-        copies.start(ar_p.at[x, y], ar_p.at[x, y], at_xy(a, b)) for a, b in plane
-    ]
+    ar_p[x, y, c] = total
+    plane = [(a, b, d) for a in (2, 1, 3, 0) for b in (2, 1, 3, 0) for d in (0, 1) if a or b or d]
+    mine_p = ar_p.at[x, y, c]
+    ar_in = [copies.start(mine_p, mine_p, at_xy(a, b, d)) for a, b, d in plane]
     for o, n in zip(offs, zp_in):
         copies.arrived(n, zp_r.at[turn(y, 4 - o)])
 
@@ -697,11 +694,13 @@
         dvalue[:, start : start + VP] = jnp.where(lane < VD, even, odd).astype(bf16)
         dvalue[:, start + VP : start + VP + 128] = odd[:, 0:128].astype(bf16)
 
-    for (a, b), n in zip(plane, ar_in):
-        copies.arrived(n, ar_p.at[turn(x, 4 - a), turn(y, 4 - b)])
+    for (a, b, d), n in zip(plane, ar_in):
+        from_core = 1 - c if d else c
+        copies.arrived(n, ar_p.at[turn(x, 4 - a), turn(y, 4 - b), from_core])
     total = jnp.zeros((1, ROW), f32)
     for a in range(4):
-        total = total + ((ar_p[a, 0] + ar_p[a, 1]) + (ar_p[a, 2] + ar_p[a, 3]))
+        for b in range(4):
+            total = total + (ar_p[a, b, 0] + ar_p[a, b, 1])
     dgain[...] = total[:, 0:C]
     loss_out[...] = total[:, C:]
     copies.finish()
@@ -794,8 +793,7 @@
         V((ROWS, C), f32),
         V((ROWS, C), f32),
         V((1, C), f32),
-        V((2, 1, ROW), f32),
-        V((4, 4, 1, ROW), f32),
+        V((4, 4, 2, 1, ROW), f32),
         V((16, 1, ROW), f32),
         pltpu.SemaphoreType.DMA((COPIES,)),
         pltpu.SemaphoreType.DMA((COPIES,)),

time: 71.1 us -> 71 us (level)
  no operation moved by 1% of the time
where the time goes in v5:
time: 71 us; the launch traced here: 70.9 us
  Pallas kernels  70.2 us (99%)
    pallas_call x1, Pallas kernels, body(): pl.pallas_call(step_kernel, name='strand_step', out_shape=(out((ROWS, C),...  69.3 us

profile of v5, /device:TPU:1, one launch (start us, length us, event | category | flops | bytes accessed | tf_op | source)
XLA Modules:
  0.0 70.9 jit_solution(6384808064428441391)
XLA Ops:
  0.6 69.3 %strand_step.1 = (bf16[256,1024]{1,0:T(8,128)(2,1)S(1)}, bf16[32,512]{1,0:T(8,128)(2,1)S(1)}, bf16[32,512]{1,0:T(8,128)(2,1)S(1)}, bf16[32,768]{1,0:T(8,128)(2,1...) custom-call(bf16[256,1024]{1,0:T(8,128)(2,1)} %bitcast.18, s32[1,16]{1,0:T(1,128)} %bitcast.26, ...), custom_call_target="tpu_custom_call" | custom-call | tf_op jit(solution)/shard_map/strand_step/pallas_call | solution.py:803
  70.0 0.9 %store.1 = (bf16[256,1024]{1,0:T(8,128)(2,1)}, bf16[32,512]{1,0:T(8,128)(2,1)}, bf16[32,512]{1,0:T(8,128)(2,1)}, bf16[32,768]{1,0:T(8,128)(2,1)}, f32[1,1024]{1,0:T(1,128)}, /*index=5*/f32[1,128]{1,0:T(1,128)}) custom-call(bf16[256,1024]{1,0:T(8,128)(2,1)S(1)} %get-tuple-element.18.refs_0_, bf16[32,512]{1,0:T(8,128)(2,1)S(1)} %get-tuple-element.19.refs_1_, ...), custom_call_target="tpu_custom_call" | custom-call | tf_op jit(solution)/shard_map/store/pallas_call | solution.py:838
